TPU v7x, 256 devices: a whole 4x4x8 slice. The times are simulated.
256 devices in a mesh: tm: 4 (over x), space: 64 (over z, y, core).
Axes of the slice: x: 4, y: 4, z: 8, core: 2. Of those that a mesh axis runs over, the one named last changes fastest.
Arguments:
- residual: float32 [64, 512, 8, 128], P('tm', 'space'), may hold values from -24 to 24
- capacity: float32 [512, 8, 128], P('space'), may hold values from 0.25 to 4
Outputs:
- preconditioned: float32 [64, 512, 8, 128], P('tm', 'space')
All inputs are finite; a program needn't handle non-finite values.
Results may differ from a plain program's by a relative error of at most 0.0003.
Values sent between devices are 32-bit elements; how exact they have to be, the bound alone decides.
A program may use at most 64 MiB of HBM per device.

v0:
```python
import math

import jax
import jax.numpy as jnp
from jax import lax
from jax.sharding import PartitionSpec as P

GRID_DEPTH = 4
SMOOTH = 2
COARSE_SWEEPS = 6


ALPHA_CORNER = 0.01
STEP_SIZE = 0.5
DIFFUSE = 2.0
ADVECT = (0.2, -0.15, 0.1)
OMEGA = 0.7
HIGHEST = lax.Precision.HIGHEST


def extended(array, sides, width):
    for axis, dim in sides:
        peers, length = (lax.axis_size(axis), array.shape[dim])
        up = [(i, (i + 1) % peers) for i in range(peers - 1)]
        down = [(j, i) for i, j in up]
        last = lax.slice_in_dim(array, length - width, length, axis=dim)
        initial = lax.slice_in_dim(array, 0, width, axis=dim)
        before = lax.ppermute(last, axis, up)
        after = lax.ppermute(initial, axis, down)
        array = jnp.concatenate([before, array, after], axis=dim)
    return array


def level_coefficients(per_level_values):
    spread = DIFFUSE / 4.0**per_level_values
    drifts = tuple((component / 2.0**per_level_values for component in ADVECT))
    return (spread, drifts)


def pad_second(volume, position):
    widths = [(0, 0)] * volume.ndim
    widths[position] = (1, 1)
    return jnp.pad(volume, widths)


def apply_operator(padded, current_capacity, spectral_shifts, per_level_values):
    spread, drifts = level_coefficients(per_level_values)
    centre = padded[:, :, 1:-1]
    upper_first = padded[:, :, 2:]
    lower_first = padded[:, :, :-2]
    wide_second = pad_second(centre, 3)
    upper_second = wide_second[:, :, :, 2:]
    lower_second = wide_second[:, :, :, :-2]
    wide_third = pad_second(centre, 4)
    upper_third = wide_third[:, :, :, :, 2:]
    lower_third = wide_third[:, :, :, :, :-2]
    stencil = spread * (
        6.0 * centre
        - upper_first
        - lower_first
        - upper_second
        - lower_second
        - upper_third
        - lower_third
    )
    stencil = (
        stencil
        + drifts[0] * (upper_first - lower_first)
        + drifts[1] * (upper_second - lower_second)
        + drifts[2] * (upper_third - lower_third)
    )
    first_shift, second_shift, third_shift = spectral_shifts
    real_part = centre[0]
    imag_part = centre[1]
    shifted = jnp.stack(
        [
            current_capacity * (first_shift * real_part - second_shift * imag_part),
            current_capacity * (second_shift * real_part + third_shift * imag_part),
        ]
    )
    return stencil + shifted


def inverse_diagonal(current_capacity, spectral_shifts, per_level_values):
    spread, drifts = level_coefficients(per_level_values)
    first_shift, second_shift, third_shift = spectral_shifts
    top_left = current_capacity * first_shift + 6.0 * spread
    coupling = current_capacity * second_shift
    bottom_right = current_capacity * third_shift + 6.0 * spread
    determinant = top_left * bottom_right + coupling * coupling
    return (bottom_right / determinant, coupling / determinant, top_left / determinant)


def damped_update(residual_now, inverse):
    diagonal_a, diagonal_b, diagonal_c = inverse
    return OMEGA * jnp.stack(
        [
            diagonal_a * residual_now[0] + diagonal_b * residual_now[1],
            diagonal_c * residual_now[1] - diagonal_b * residual_now[0],
        ]
    )


def restrict_to_coarse(volume):
    leading = volume.shape[:-3]
    first_extent, second_extent, third_extent = volume.shape[-3:]
    blocks = volume.reshape(
        leading + (first_extent // 2, 2, second_extent // 2, 2, third_extent // 2, 2)
    )
    lead_count = len(leading)
    return jnp.mean(blocks, axis=(lead_count + 1, lead_count + 3, lead_count + 5))


def prolong_cells(volume):
    leading = volume.shape[:-3]
    first_extent, second_extent, third_extent = volume.shape[-3:]
    expanded = jnp.broadcast_to(
        volume[..., :, None, :, None, :, None],
        leading + (first_extent, 2, second_extent, 2, third_extent, 2),
    )
    return expanded.reshape(leading + (2 * first_extent, 2 * second_extent, 2 * third_extent))


def shift_values(frequency, length):
    ratio_step = ALPHA_CORNER ** (1.0 / length)
    phases = 2.0 * math.pi / length * frequency.astype(jnp.float32)
    first_shift = (1.0 - ratio_step * jnp.cos(phases)) / STEP_SIZE
    second_shift = ratio_step * jnp.sin(phases) / STEP_SIZE
    leading = frequency == 0
    second_shift = jnp.where(leading, 0.0, second_shift)
    third_shift = jnp.where(leading, (1.0 + ratio_step) / STEP_SIZE, first_shift)
    return tuple(
        (column.reshape(-1, 1, 1, 1) for column in (first_shift, second_shift, third_shift))
    )


def phase_grid(row_count, length):
    integers = (
        jnp.arange(row_count, dtype=jnp.int32)[:, None]
        * jnp.arange(length, dtype=jnp.int32)[None, :]
        % length
    )
    return 2.0 * math.pi / length * integers.astype(jnp.float32)


def pad_faces(volume):
    return extended(volume, (("space", 2),), 1)


def multigrid_cycle(
    per_level_values,
    forcing_term,
    capacity_fields,
    spectral_shifts,
    shared_values,
    assemble_level,
    assemble_parts,
):
    current_capacity = capacity_fields[per_level_values]
    inverse = inverse_diagonal(current_capacity, spectral_shifts, per_level_values)
    coarsest = per_level_values == GRID_DEPTH - 1
    current = damped_update(forcing_term, inverse)
    for repeat in range((COARSE_SWEEPS if coarsest else SMOOTH) - 1):
        current = current + damped_update(
            forcing_term
            - apply_operator(
                pad_faces(current), current_capacity, spectral_shifts, per_level_values
            ),
            inverse,
        )
    if coarsest:
        return current
    coarse_right_hand = restrict_to_coarse(
        forcing_term
        - apply_operator(pad_faces(current), current_capacity, spectral_shifts, per_level_values)
    )
    coarse_solution = multigrid_cycle(
        per_level_values + 1,
        coarse_right_hand,
        capacity_fields,
        spectral_shifts,
        shared_values,
        assemble_level,
        assemble_parts,
    )
    current = current + prolong_cells(coarse_solution)
    for repeat in range(SMOOTH):
        current = current + damped_update(
            forcing_term
            - apply_operator(
                pad_faces(current), current_capacity, spectral_shifts, per_level_values
            ),
            inverse,
        )
    return current


def on_device(residual, capacity):
    steps_here, thickness, extent_second, extent_third = residual.shape
    length = lax.axis_size("tm") * steps_here
    ratio_step = ALPHA_CORNER ** (1.0 / length)
    moments = (lax.axis_index("tm") * steps_here + jnp.arange(steps_here, dtype=jnp.int32)).astype(
        jnp.float32
    )
    scaled = (residual * jnp.power(ratio_step, moments)[:, None, None, None]).reshape(
        steps_here, -1
    )
    series = lax.all_to_all(scaled, "tm", split_axis=1, concat_axis=0, tiled=True)
    all_weights = jnp.power(ratio_step, jnp.arange(length, dtype=jnp.float32))
    alternate = 1.0 - 2.0 * (jnp.arange(length, dtype=jnp.int32) % 2).astype(jnp.float32)
    capacity_fields = [capacity]
    for per_level_values in range(1, GRID_DEPTH):
        capacity_fields.append(restrict_to_coarse(capacity_fields[-1]))
    halves = length // 2
    phases = phase_grid(halves, length)
    first_row = jnp.arange(halves, dtype=jnp.int32)[:, None] == 0
    forward = jnp.concatenate(
        [jnp.cos(phases), jnp.where(first_row, alternate[None, :], -jnp.sin(phases))], axis=0
    )
    spectrum = jnp.dot(forward, series, precision=HIGHEST).reshape(2, halves, -1)
    received = lax.all_to_all(spectrum, "tm", split_axis=1, concat_axis=2, tiled=True)
    slot_count = steps_here // 2
    frequency = lax.axis_index("tm") * slot_count + jnp.arange(slot_count, dtype=jnp.int32)
    spectral_shifts = shift_values(frequency, length)
    field_list = received.reshape(2, slot_count, thickness, extent_second, extent_third)
    solved_fields = multigrid_cycle(
        0, field_list, capacity_fields, spectral_shifts, False, GRID_DEPTH, None
    )
    flattened = solved_fields.reshape(2, slot_count, -1)
    returned = lax.all_to_all(flattened, "tm", split_axis=2, concat_axis=1, tiled=True)
    halves = length // 2
    phases = jnp.transpose(phase_grid(halves, length))
    first_column = jnp.arange(halves, dtype=jnp.int32)[None, :] == 0
    real_columns = jnp.where(first_column, 1.0, 2.0 * jnp.cos(phases)) / length
    imag_columns = jnp.where(first_column, alternate[:, None], -2.0 * jnp.sin(phases)) / length
    inverse_table = jnp.concatenate([real_columns, imag_columns], axis=1)
    values = jnp.dot(
        inverse_table,
        returned.reshape(returned.shape[0] * returned.shape[1], -1),
        precision=HIGHEST,
    )
    values = values / all_weights[:, None]
    result = lax.all_to_all(values, "tm", split_axis=0, concat_axis=1, tiled=True)
    return result.reshape(residual.shape)


def solution(mesh):
    return jax.shard_map(
        on_device,
        mesh=mesh,
        in_specs=(P("tm", "space", None, None), P("space", None, None)),
        out_specs=P("tm", "space", None, None),
        check_vma=False,
    )
```

profile of v0, /device:TPU:128, one launch (start us, length us, event | category | flops | bytes accessed | tf_op | source)
XLA Modules:
  0.0 334.7 jit_solution(5365894901311721155)
XLA Ops:
  2.5 4.3 %all-to-all-start = ((f32[16,4,2048]{2,0,1:T(8,128)}), f32[16,4,2048]{2,0,1:T(8,128)S(1)}, u32[]{:S(2)}, u32[]{:S(2)}) async-start(f32[16,4,2048]{2,0,1:T(8,128)} %copy.706), calls=%async_computation | async-start | bytes 1048576 | tf_op jit(solution)/shard_map/all_to_all | solution.py:208
  10.6 5.7 %all-to-all-done = f32[16,4,2048]{2,0,1:T(8,128)S(1)} async-done(((f32[16,4,2048]{2,0,1:T(8,128)}), f32[16,4,2048]{2,0,1:T(8,128)S(1)}, u32[]{:S(2)}, u32[]{:S(2)}) %all-to-all-start) | async-done | bytes 524320 | tf_op jit(solution)/shard_map/all_to_all | solution.py:208
  21.6 8.2 %all-to-all-done.1 = f32[2,32,2048]{2,0,1:T(2,128)S(1)} async-done(((f32[2,32,2048]{2,0,1:T(2,128)}), f32[2,32,2048]{2,0,1:T(2,128)S(1)}, u32[]{:S(2)}, u32[]{:S(2)}) %all-to-all-start.1) | async-done | bytes 524320 | tf_op jit(solution)/shard_map/all_to_all | solution.py:221
  36.9 5.1 %collective-permute-done.1 = f32[2,8,1,8,128]{4,3,2,1,0:T(8,128)S(1)} collective-permute-done((f32[2,8,1,8,128]{4,3,2,1,0:T(8,128)S(1)}, f32[2,8,1,8,128]{4,3,2,1,0:T(8,128)S(1)}, u32[]{:S(2)}, u32[]{:S(2)}) %collective-permute-start.1) | collective-permute-done | bytes 65568 | tf_op jit(solution)/shard_map/ppermute | solution.py:28
  49.0 4.7 %collective-permute-done.3 = f32[2,8,1,8,128]{4,3,2,1,0:T(8,128)S(1)} collective-permute-done((f32[2,8,1,8,128]{4,3,2,1,0:T(8,128)S(1)}, f32[2,8,1,8,128]{4,3,2,1,0:T(8,128)S(1)}, u32[]{:S(2)}, u32[]{:S(2)}) %collective-permute-start.3) | collective-permute-done | bytes 65568 | tf_op jit(solution)/shard_map/ppermute | solution.py:28
  55.6 4.7 %copy.709 = f32[2,8,8,8,128]{1,4,3,2,0:T(8,128)} copy(f32[2,8,8,8,128]{4,3,2,1,0:T(8,128)S(1)} %fusion.6) | data formatting | bytes 1048576 | tf_op jit(solution)/shard_map/sub | solution.py:174
  60.3 8.8 %reduce_sum.69 = f32[2,8,4,4,64]{1,4,3,2,0:T(8,128)S(1)} reduce(f32[2,8,4,2,4,2,64,2]{1,7,6,5,4,3,2,0:T(2,128)} %bitcast.76, f32[]{:T(128)} %constant.135.clone.1), dimensions={3,5,7}, to_apply=%region_1.2 | reduce | flops 114688 | bytes 589828 | tf_op jit(solution)/shard_map/reduce_sum | solution.py:111
  74.0 6.0 %collective-permute-done.5 = f32[2,8,1,4,64]{4,1,3,2,0:T(8,128)S(1)} collective-permute-done((f32[2,8,1,4,64]{4,1,3,2,0:T(8,128)S(1)}, f32[2,8,1,4,64]{4,1,3,2,0:T(8,128)S(1)}, u32[]{:S(2)}, u32[]{:S(2)}) %collective-permute-start.5) | collective-permute-done | bytes 16416 | tf_op jit(solution)/shard_map/ppermute | solution.py:28
  84.8 6.0 %collective-permute-done.7 = f32[2,8,1,4,64]{4,1,3,2,0:T(8,128)S(1)} collective-permute-done((f32[2,8,1,4,64]{4,1,3,2,0:T(8,128)S(1)}, f32[2,8,1,4,64]{4,1,3,2,0:T(8,128)S(1)}, u32[]{:S(2)}, u32[]{:S(2)}) %collective-permute-start.7) | collective-permute-done | bytes 16416 | tf_op jit(solution)/shard_map/ppermute | solution.py:28
  99.9 5.9 %collective-permute-done.9 = f32[2,8,1,2,32]{4,1,3,2,0:T(8,128)S(1)} collective-permute-done((f32[2,8,1,2,32]{4,1,3,2,0:T(8,128)S(1)}, f32[2,8,1,2,32]{4,1,3,2,0:T(8,128)S(1)}, u32[]{:S(2)}, u32[]{:S(2)}) %collective-permute-start.9) | collective-permute-done | bytes 4128 | tf_op jit(solution)/shard_map/ppermute | solution.py:28
  110.4 5.9 %collective-permute-done.11 = f32[2,8,1,2,32]{4,1,3,2,0:T(8,128)S(1)} collective-permute-done((f32[2,8,1,2,32]{4,1,3,2,0:T(8,128)S(1)}, f32[2,8,1,2,32]{4,1,3,2,0:T(8,128)S(1)}, u32[]{:S(2)}, u32[]{:S(2)}) %collective-permute-start.11) | collective-permute-done | bytes 4128 | tf_op jit(solution)/shard_map/ppermute | solution.py:28
  121.1 5.8 %collective-permute-done.13 = f32[2,8,1,1,16]{4,1,3,2,0:T(8,128)S(1)} collective-permute-done((f32[2,8,1,1,16]{4,1,3,2,0:T(8,128)S(1)}, f32[2,8,1,1,16]{4,1,3,2,0:T(8,128)S(1)}, u32[]{:S(2)}, u32[]{:S(2)}) %collective-permute-start.13) | collective-permute-done | bytes 1056 | tf_op jit(solution)/shard_map/ppermute | solution.py:28
  131.5 5.8 %collective-permute-done.15 = f32[2,8,1,1,16]{4,1,3,2,0:T(8,128)S(1)} collective-permute-done((f32[2,8,1,1,16]{4,1,3,2,0:T(8,128)S(1)}, f32[2,8,1,1,16]{4,1,3,2,0:T(8,128)S(1)}, u32[]{:S(2)}, u32[]{:S(2)}) %collective-permute-start.15) | collective-permute-done | bytes 1056 | tf_op jit(solution)/shard_map/ppermute | solution.py:28
  141.9 5.8 %collective-permute-done.17 = f32[2,8,1,1,16]{4,1,3,2,0:T(8,128)S(1)} collective-permute-done((f32[2,8,1,1,16]{4,1,3,2,0:T(8,128)S(1)}, f32[2,8,1,1,16]{4,1,3,2,0:T(8,128)S(1)}, u32[]{:S(2)}, u32[]{:S(2)}) %collective-permute-start.17) | collective-permute-done | bytes 1056 | tf_op jit(solution)/shard_map/ppermute | solution.py:28
  152.3 5.8 %collective-permute-done.19 = f32[2,8,1,1,16]{4,1,3,2,0:T(8,128)S(1)} collective-permute-done((f32[2,8,1,1,16]{4,1,3,2,0:T(8,128)S(1)}, f32[2,8,1,1,16]{4,1,3,2,0:T(8,128)S(1)}, u32[]{:S(2)}, u32[]{:S(2)}) %collective-permute-start.19) | collective-permute-done | bytes 1056 | tf_op jit(solution)/shard_map/ppermute | solution.py:28
  162.7 5.8 %collective-permute-done.21 = f32[2,8,1,1,16]{4,1,3,2,0:T(8,128)S(1)} collective-permute-done((f32[2,8,1,1,16]{4,1,3,2,0:T(8,128)S(1)}, f32[2,8,1,1,16]{4,1,3,2,0:T(8,128)S(1)}, u32[]{:S(2)}, u32[]{:S(2)}) %collective-permute-start.21) | collective-permute-done | bytes 1056 | tf_op jit(solution)/shard_map/ppermute | solution.py:28
  173.3 5.9 %collective-permute-done.23 = f32[2,8,1,2,32]{4,1,3,2,0:T(8,128)S(1)} collective-permute-done((f32[2,8,1,2,32]{4,1,3,2,0:T(8,128)S(1)}, f32[2,8,1,2,32]{4,1,3,2,0:T(8,128)S(1)}, u32[]{:S(2)}, u32[]{:S(2)}) %collective-permute-start.23) | collective-permute-done | bytes 4128 | tf_op jit(solution)/shard_map/ppermute | solution.py:28
  183.9 5.9 %collective-permute-done.25 = f32[2,8,1,2,32]{4,1,3,2,0:T(8,128)S(1)} collective-permute-done((f32[2,8,1,2,32]{4,1,3,2,0:T(8,128)S(1)}, f32[2,8,1,2,32]{4,1,3,2,0:T(8,128)S(1)}, u32[]{:S(2)}, u32[]{:S(2)}) %collective-permute-start.25) | collective-permute-done | bytes 4128 | tf_op jit(solution)/shard_map/ppermute | solution.py:28
  197.0 6.0 %collective-permute-done.27 = f32[2,8,1,4,64]{4,1,3,2,0:T(8,128)S(1)} collective-permute-done((f32[2,8,1,4,64]{4,1,3,2,0:T(8,128)S(1)}, f32[2,8,1,4,64]{4,1,3,2,0:T(8,128)S(1)}, u32[]{:S(2)}, u32[]{:S(2)}) %collective-permute-start.27) | collective-permute-done | bytes 16416 | tf_op jit(solution)/shard_map/ppermute | solution.py:28
  208.0 5.8 %collective-permute-done.29 = f32[2,8,1,4,64]{4,1,3,2,0:T(8,128)S(1)} collective-permute-done((f32[2,8,1,4,64]{4,1,3,2,0:T(8,128)S(1)}, f32[2,8,1,4,64]{4,1,3,2,0:T(8,128)S(1)}, u32[]{:S(2)}, u32[]{:S(2)}) %collective-permute-start.29) | collective-permute-done | bytes 16416 | tf_op jit(solution)/shard_map/ppermute | solution.py:28
  214.5 7.5 %broadcast_in_dim.62 = f32[2,8,4,2,4,2,64,2]{1,7,6,5,4,3,2,0:T(2,128)} broadcast(f32[2,8,4,4,64]{1,4,3,2,0:T(8,128)S(1)} %copy.719), dimensions={0,1,2,4,6} | broadcast | bytes 589824 | tf_op jit(solution)/shard_map/broadcast_in_dim | solution.py:117
  222.0 5.1 %copy.721 = f32[2,8,8,8,128]{4,3,2,1,0:T(8,128)S(1)} copy(f32[2,8,8,8,128]{1,4,3,2,0:T(8,128)} %bitcast.74) | data formatting | bytes 1048576 | tf_op jit(solution)/shard_map/reshape | solution.py:121
  231.8 5.4 %copy.720 = f32[2,8,8192]{2,1,0:T(8,128)S(1)} copy(f32[2,8,8192]{1,2,0:T(8,128)} %bitcast.75) | data formatting | bytes 1048576 | tf_op jit(solution)/shard_map/reshape | solution.py:121
  239.0 5.6 %collective-permute-start.32 = (f32[2,8,1,8,128]{4,3,2,1,0:T(8,128)S(1)}, f32[2,8,1,8,128]{4,3,2,1,0:T(8,128)S(1)}, u32[]{:S(2)}, u32[]{:S(2)}) collective-permute-start(f32[2,8,1,8,128]{4,3,2,1,0:T(8,128)S(1)} %get-tuple-element.23), channel_id=1, source_target_pairs={{1,0},{2,1},{3,2},{4,3},{5,4},{6,5},{7,6},{8,7},{9,8},{10,9},{11,1... | collective-permute-start | bytes 196616 | tf_op jit(solution)/shard_map/ppermute | solution.py:29
  248.1 5.3 %collective-permute-done.33 = f32[2,8,1,8,128]{4,3,2,1,0:T(8,128)S(1)} collective-permute-done((f32[2,8,1,8,128]{4,3,2,1,0:T(8,128)S(1)}, f32[2,8,1,8,128]{4,3,2,1,0:T(8,128)S(1)}, u32[]{:S(2)}, u32[]{:S(2)}) %collective-permute-start.33) | collective-permute-done | bytes 65568 | tf_op jit(solution)/shard_map/ppermute | solution.py:28
  257.1 7.8 %copy.722 = f32[2,8,8192]{1,0,2:T(2,128)} copy(f32[2,8,8192]{2,1,0:T(8,128)S(1)} %fusion.3) | data formatting | bytes 1048576 | tf_op jit(solution)/shard_map/add | solution.py:188
  265.0 15.6 %reshape.2439 = f32[4,1,32768]{2,1,0:T(1,128)} reshape(f32[8192,2,8]{2,1,0:T(2,128)} %bitcast.77) | data formatting | bytes 1048576
  280.6 3.7 %all-to-all-start.2 = ((f32[4,1,32768]{2,1,0:T(1,128)}), f32[4,1,32768]{2,1,0:T(1,128)S(1)}, u32[]{:S(2)}, u32[]{:S(2)}) async-start(f32[4,1,32768]{2,1,0:T(1,128)} %reshape.2439), calls=%async_computation.2 | async-start | bytes 1048576 | tf_op jit(solution)/shard_map/all_to_all | solution.py:230
  284.5 7.9 %all-to-all-done.2 = f32[4,1,32768]{2,1,0:T(1,128)S(1)} async-done(((f32[4,1,32768]{2,1,0:T(1,128)}), f32[4,1,32768]{2,1,0:T(1,128)S(1)}, u32[]{:S(2)}, u32[]{:S(2)}) %all-to-all-start.2) | async-done | bytes 524320 | tf_op jit(solution)/shard_map/all_to_all | solution.py:230
  295.0 16.2 %reshape.2440 = f32[8192,2,8]{2,1,0:T(2,128)} reshape(f32[4,32768]{1,0:T(4,128)S(1)} %reduce.6) | data formatting | bytes 1048576
  311.2 10.2 %copy.726 = f32[2,8,4,2048]{3,2,1,0:T(4,128)S(1)} copy(f32[2,8,4,2048]{1,0,3,2:T(2,128)} %bitcast.78) | data formatting | bytes 1048576 | tf_op jit(solution)/shard_map/all_to_all | solution.py:230
  322.3 10.5 %all_to_all.65 = f32[4,16,2048]{2,1,0:T(8,128)S(1)} all-to-all(f32[4,16,2048]{2,1,0:T(8,128)S(1)} %bitcast.89), channel_id=1, replica_groups=mesh['tm'=4,'space'=64] {'tm'}, dimensions={0} | all-to-all | bytes 1048576 | tf_op jit(solution)/shard_map/all_to_all | solution.py:243
  (205 shorter events, 114.6 us)
Async XLA Ops:
  2.5 13.8 %all-to-all-start = ((f32[16,4,2048]{2,0,1:T(8,128)}), f32[16,4,2048]{2,0,1:T(8,128)S(1)}, u32[]{:S(2)}, u32[]{:S(2)}) async-start(f32[16,4,2048]{2,0,1:T(8,128)} %copy.706), calls=%async_computation | async-start | bytes 1048576 | tf_op jit(solution)/shard_map/all_to_all | solution.py:208
  18.0 11.8 %all-to-all-start.1 = ((f32[2,32,2048]{2,0,1:T(2,128)}), f32[2,32,2048]{2,0,1:T(2,128)S(1)}, u32[]{:S(2)}, u32[]{:S(2)}) async-start(f32[2,32,2048]{2,0,1:T(2,128)} %copy.707), calls=%async_computation.1 | async-start | bytes 1048576 | tf_op jit(solution)/shard_map/all_to_all | solution.py:221
  31.2 5.7 %collective-permute-start = (f32[2,8,1,8,128]{4,3,2,1,0:T(8,128)S(1)}, f32[2,8,1,8,128]{4,3,2,1,0:T(8,128)S(1)}, u32[]{:S(2)}, u32[]{:S(2)}) collective-permute-start(f32[2,8,1,8,128]{4,3,2,1,0:T(8,128)S(1)} %get-tuple-element.29), channel_id=1, source_target_pairs={{1,0},{2,1},{3,2},{4,3},{5,4},{6,5},{7,6},{8,7},{9,8},{10,9},{11,1... | collective-permute-start | bytes 196616 | tf_op jit(solution)/shard_map/ppermute | solution.py:29
  33.1 8.9 %collective-permute-start.1 = (f32[2,8,1,8,128]{4,3,2,1,0:T(8,128)S(1)}, f32[2,8,1,8,128]{4,3,2,1,0:T(8,128)S(1)}, u32[]{:S(2)}, u32[]{:S(2)}) collective-permute-start(f32[2,8,1,8,128]{4,3,2,1,0:T(8,128)S(1)} %get-tuple-element.30), channel_id=1, source_target_pairs={{0,1},{1,2},{2,3},{3,4},{4,5},{5,6},{6,7},{7,8},{8,9},{9,10},{10,1... | collective-permute-start | bytes 196616 | tf_op jit(solution)/shard_map/ppermute | solution.py:28
  42.9 6.2 %collective-permute-start.2 = (f32[2,8,1,8,128]{4,3,2,1,0:T(8,128)S(1)}, f32[2,8,1,8,128]{4,3,2,1,0:T(8,128)S(1)}, u32[]{:S(2)}, u32[]{:S(2)}) collective-permute-start(f32[2,8,1,8,128]{4,3,2,1,0:T(8,128)S(1)} %get-tuple-element.27), channel_id=1, source_target_pairs={{1,0},{2,1},{3,2},{4,3},{5,4},{6,5},{7,6},{8,7},{9,8},{10,9},{11,1... | collective-permute-start | bytes 196616 | tf_op jit(solution)/shard_map/ppermute | solution.py:29
  44.8 8.9 %collective-permute-start.3 = (f32[2,8,1,8,128]{4,3,2,1,0:T(8,128)S(1)}, f32[2,8,1,8,128]{4,3,2,1,0:T(8,128)S(1)}, u32[]{:S(2)}, u32[]{:S(2)}) collective-permute-start(f32[2,8,1,8,128]{4,3,2,1,0:T(8,128)S(1)} %get-tuple-element.28), channel_id=1, source_target_pairs={{0,1},{1,2},{2,3},{3,4},{4,5},{5,6},{6,7},{7,8},{8,9},{9,10},{10,1... | collective-permute-start | bytes 196616 | tf_op jit(solution)/shard_map/ppermute | solution.py:28
  69.6 4.4 %collective-permute-start.4 = (f32[2,8,1,4,64]{4,1,3,2,0:T(8,128)S(1)}, f32[2,8,1,4,64]{4,1,3,2,0:T(8,128)S(1)}, u32[]{:S(2)}, u32[]{:S(2)}) collective-permute-start(f32[2,8,1,4,64]{4,1,3,2,0:T(8,128)S(1)} %get-tuple-element.55), channel_id=1, source_target_pairs={{1,0},{2,1},{3,2},{4,3},{5,4},{6,5},{7,6},{8,7},{9,8},{10,9},{11,1... | collective-permute-start | bytes 49160 | tf_op jit(solution)/shard_map/ppermute | solution.py:29
  71.5 8.6 %collective-permute-start.5 = (f32[2,8,1,4,64]{4,1,3,2,0:T(8,128)S(1)}, f32[2,8,1,4,64]{4,1,3,2,0:T(8,128)S(1)}, u32[]{:S(2)}, u32[]{:S(2)}) collective-permute-start(f32[2,8,1,4,64]{4,1,3,2,0:T(8,128)S(1)} %get-tuple-element.56), channel_id=1, source_target_pairs={{0,1},{1,2},{2,3},{3,4},{4,5},{5,6},{6,7},{7,8},{8,9},{9,10},{10,1... | collective-permute-start | bytes 49160 | tf_op jit(solution)/shard_map/ppermute | solution.py:28
  80.4 4.4 %collective-permute-start.6 = (f32[2,8,1,4,64]{4,1,3,2,0:T(8,128)S(1)}, f32[2,8,1,4,64]{4,1,3,2,0:T(8,128)S(1)}, u32[]{:S(2)}, u32[]{:S(2)}) collective-permute-start(f32[2,8,1,4,64]{4,1,3,2,0:T(8,128)S(1)} %get-tuple-element.53), channel_id=1, source_target_pairs={{1,0},{2,1},{3,2},{4,3},{5,4},{6,5},{7,6},{8,7},{9,8},{10,9},{11,1... | collective-permute-start | bytes 49160 | tf_op jit(solution)/shard_map/ppermute | solution.py:29
  82.3 8.6 %collective-permute-start.7 = (f32[2,8,1,4,64]{4,1,3,2,0:T(8,128)S(1)}, f32[2,8,1,4,64]{4,1,3,2,0:T(8,128)S(1)}, u32[]{:S(2)}, u32[]{:S(2)}) collective-permute-start(f32[2,8,1,4,64]{4,1,3,2,0:T(8,128)S(1)} %get-tuple-element.54), channel_id=1, source_target_pairs={{0,1},{1,2},{2,3},{3,4},{4,5},{5,6},{6,7},{7,8},{8,9},{9,10},{10,1... | collective-permute-start | bytes 49160 | tf_op jit(solution)/shard_map/ppermute | solution.py:28
  95.5 4.4 %collective-permute-start.8 = (f32[2,8,1,2,32]{4,1,3,2,0:T(8,128)S(1)}, f32[2,8,1,2,32]{4,1,3,2,0:T(8,128)S(1)}, u32[]{:S(2)}, u32[]{:S(2)}) collective-permute-start(f32[2,8,1,2,32]{4,1,3,2,0:T(8,128)S(1)} %get-tuple-element.79), channel_id=1, source_target_pairs={{1,0},{2,1},{3,2},{4,3},{5,4},{6,5},{7,6},{8,7},{9,8},{10,9},{11,1... | collective-permute-start | bytes 12296 | tf_op jit(solution)/shard_map/ppermute | solution.py:29
  97.4 8.4 %collective-permute-start.9 = (f32[2,8,1,2,32]{4,1,3,2,0:T(8,128)S(1)}, f32[2,8,1,2,32]{4,1,3,2,0:T(8,128)S(1)}, u32[]{:S(2)}, u32[]{:S(2)}) collective-permute-start(f32[2,8,1,2,32]{4,1,3,2,0:T(8,128)S(1)} %get-tuple-element.80), channel_id=1, source_target_pairs={{0,1},{1,2},{2,3},{3,4},{4,5},{5,6},{6,7},{7,8},{8,9},{9,10},{10,1... | collective-permute-start | bytes 12296 | tf_op jit(solution)/shard_map/ppermute | solution.py:28
  106.0 4.4 %collective-permute-start.10 = (f32[2,8,1,2,32]{4,1,3,2,0:T(8,128)S(1)}, f32[2,8,1,2,32]{4,1,3,2,0:T(8,128)S(1)}, u32[]{:S(2)}, u32[]{:S(2)}) collective-permute-start(f32[2,8,1,2,32]{4,1,3,2,0:T(8,128)S(1)} %get-tuple-element.77), channel_id=1, source_target_pairs={{1,0},{2,1},{3,2},{4,3},{5,4},{6,5},{7,6},{8,7},{9,8},{10,9},{11,1... | collective-permute-start | bytes 12296 | tf_op jit(solution)/shard_map/ppermute | solution.py:29
  107.9 8.4 %collective-permute-start.11 = (f32[2,8,1,2,32]{4,1,3,2,0:T(8,128)S(1)}, f32[2,8,1,2,32]{4,1,3,2,0:T(8,128)S(1)}, u32[]{:S(2)}, u32[]{:S(2)}) collective-permute-start(f32[2,8,1,2,32]{4,1,3,2,0:T(8,128)S(1)} %get-tuple-element.78), channel_id=1, source_target_pairs={{0,1},{1,2},{2,3},{3,4},{4,5},{5,6},{6,7},{7,8},{8,9},{9,10},{10,1... | collective-permute-start | bytes 12296 | tf_op jit(solution)/shard_map/ppermute | solution.py:28
  118.6 8.3 %collective-permute-start.13 = (f32[2,8,1,1,16]{4,1,3,2,0:T(8,128)S(1)}, f32[2,8,1,1,16]{4,1,3,2,0:T(8,128)S(1)}, u32[]{:S(2)}, u32[]{:S(2)}) collective-permute-start(f32[2,8,1,1,16]{4,1,3,2,0:T(8,128)S(1)} %fusion.66), channel_id=1, source_target_pairs={{0,1},{1,2},{2,3},{3,4},{4,5},{5,6},{6,7},{7,8},{8,9},{9,10},{10,1... | collective-permute-start | bytes 3080 | tf_op jit(solution)/shard_map/ppermute | solution.py:28
  129.0 8.3 %collective-permute-start.15 = (f32[2,8,1,1,16]{4,1,3,2,0:T(8,128)S(1)}, f32[2,8,1,1,16]{4,1,3,2,0:T(8,128)S(1)}, u32[]{:S(2)}, u32[]{:S(2)}) collective-permute-start(f32[2,8,1,1,16]{4,1,3,2,0:T(8,128)S(1)} %fusion.57), channel_id=1, source_target_pairs={{0,1},{1,2},{2,3},{3,4},{4,5},{5,6},{6,7},{7,8},{8,9},{9,10},{10,1... | collective-permute-start | bytes 3080 | tf_op jit(solution)/shard_map/ppermute | solution.py:28
  139.4 8.3 %collective-permute-start.17 = (f32[2,8,1,1,16]{4,1,3,2,0:T(8,128)S(1)}, f32[2,8,1,1,16]{4,1,3,2,0:T(8,128)S(1)}, u32[]{:S(2)}, u32[]{:S(2)}) collective-permute-start(f32[2,8,1,1,16]{4,1,3,2,0:T(8,128)S(1)} %fusion.59), channel_id=1, source_target_pairs={{0,1},{1,2},{2,3},{3,4},{4,5},{5,6},{6,7},{7,8},{8,9},{9,10},{10,1... | collective-permute-start | bytes 3080 | tf_op jit(solution)/shard_map/ppermute | solution.py:28
  149.8 8.3 %collective-permute-start.19 = (f32[2,8,1,1,16]{4,1,3,2,0:T(8,128)S(1)}, f32[2,8,1,1,16]{4,1,3,2,0:T(8,128)S(1)}, u32[]{:S(2)}, u32[]{:S(2)}) collective-permute-start(f32[2,8,1,1,16]{4,1,3,2,0:T(8,128)S(1)} %fusion.61), channel_id=1, source_target_pairs={{0,1},{1,2},{2,3},{3,4},{4,5},{5,6},{6,7},{7,8},{8,9},{9,10},{10,1... | collective-permute-start | bytes 3080 | tf_op jit(solution)/shard_map/ppermute | solution.py:28
  160.2 8.3 %collective-permute-start.21 = (f32[2,8,1,1,16]{4,1,3,2,0:T(8,128)S(1)}, f32[2,8,1,1,16]{4,1,3,2,0:T(8,128)S(1)}, u32[]{:S(2)}, u32[]{:S(2)}) collective-permute-start(f32[2,8,1,1,16]{4,1,3,2,0:T(8,128)S(1)} %fusion.63), channel_id=1, source_target_pairs={{0,1},{1,2},{2,3},{3,4},{4,5},{5,6},{6,7},{7,8},{8,9},{9,10},{10,1... | collective-permute-start | bytes 3080 | tf_op jit(solution)/shard_map/ppermute | solution.py:28
  168.9 4.4 %collective-permute-start.22 = (f32[2,8,1,2,32]{4,1,3,2,0:T(8,128)S(1)}, f32[2,8,1,2,32]{4,1,3,2,0:T(8,128)S(1)}, u32[]{:S(2)}, u32[]{:S(2)}) collective-permute-start(f32[2,8,1,2,32]{4,1,3,2,0:T(8,128)S(1)} %get-tuple-element.75), channel_id=1, source_target_pairs={{1,0},{2,1},{3,2},{4,3},{5,4},{6,5},{7,6},{8,7},{9,8},{10,9},{11,1... | collective-permute-start | bytes 12296 | tf_op jit(solution)/shard_map/ppermute | solution.py:29
  170.8 8.4 %collective-permute-start.23 = (f32[2,8,1,2,32]{4,1,3,2,0:T(8,128)S(1)}, f32[2,8,1,2,32]{4,1,3,2,0:T(8,128)S(1)}, u32[]{:S(2)}, u32[]{:S(2)}) collective-permute-start(f32[2,8,1,2,32]{4,1,3,2,0:T(8,128)S(1)} %get-tuple-element.76), channel_id=1, source_target_pairs={{0,1},{1,2},{2,3},{3,4},{4,5},{5,6},{6,7},{7,8},{8,9},{9,10},{10,1... | collective-permute-start | bytes 12296 | tf_op jit(solution)/shard_map/ppermute | solution.py:28
  179.5 4.4 %collective-permute-start.24 = (f32[2,8,1,2,32]{4,1,3,2,0:T(8,128)S(1)}, f32[2,8,1,2,32]{4,1,3,2,0:T(8,128)S(1)}, u32[]{:S(2)}, u32[]{:S(2)}) collective-permute-start(f32[2,8,1,2,32]{4,1,3,2,0:T(8,128)S(1)} %get-tuple-element.73), channel_id=1, source_target_pairs={{1,0},{2,1},{3,2},{4,3},{5,4},{6,5},{7,6},{8,7},{9,8},{10,9},{11,1... | collective-permute-start | bytes 12296 | tf_op jit(solution)/shard_map/ppermute | solution.py:29
  181.4 8.4 %collective-permute-start.25 = (f32[2,8,1,2,32]{4,1,3,2,0:T(8,128)S(1)}, f32[2,8,1,2,32]{4,1,3,2,0:T(8,128)S(1)}, u32[]{:S(2)}, u32[]{:S(2)}) collective-permute-start(f32[2,8,1,2,32]{4,1,3,2,0:T(8,128)S(1)} %get-tuple-element.74), channel_id=1, source_target_pairs={{0,1},{1,2},{2,3},{3,4},{4,5},{5,6},{6,7},{7,8},{8,9},{9,10},{10,1... | collective-permute-start | bytes 12296 | tf_op jit(solution)/shard_map/ppermute | solution.py:28
  192.5 4.4 %collective-permute-start.26 = (f32[2,8,1,4,64]{4,1,3,2,0:T(8,128)S(1)}, f32[2,8,1,4,64]{4,1,3,2,0:T(8,128)S(1)}, u32[]{:S(2)}, u32[]{:S(2)}) collective-permute-start(f32[2,8,1,4,64]{4,1,3,2,0:T(8,128)S(1)} %get-tuple-element.51), channel_id=1, source_target_pairs={{1,0},{2,1},{3,2},{4,3},{5,4},{6,5},{7,6},{8,7},{9,8},{10,9},{11,1... | collective-permute-start | bytes 49160 | tf_op jit(solution)/shard_map/ppermute | solution.py:29
  194.4 8.6 %collective-permute-start.27 = (f32[2,8,1,4,64]{4,1,3,2,0:T(8,128)S(1)}, f32[2,8,1,4,64]{4,1,3,2,0:T(8,128)S(1)}, u32[]{:S(2)}, u32[]{:S(2)}) collective-permute-start(f32[2,8,1,4,64]{4,1,3,2,0:T(8,128)S(1)} %get-tuple-element.52), channel_id=1, source_target_pairs={{0,1},{1,2},{2,3},{3,4},{4,5},{5,6},{6,7},{7,8},{8,9},{9,10},{10,1... | collective-permute-start | bytes 49160 | tf_op jit(solution)/shard_map/ppermute | solution.py:28
  203.3 4.7 %collective-permute-start.28 = (f32[2,8,1,4,64]{4,1,3,2,0:T(8,128)S(1)}, f32[2,8,1,4,64]{4,1,3,2,0:T(8,128)S(1)}, u32[]{:S(2)}, u32[]{:S(2)}) collective-permute-start(f32[2,8,1,4,64]{4,1,3,2,0:T(8,128)S(1)} %get-tuple-element.49), channel_id=1, source_target_pairs={{1,0},{2,1},{3,2},{4,3},{5,4},{6,5},{7,6},{8,7},{9,8},{10,9},{11,1... | collective-permute-start | bytes 49160 | tf_op jit(solution)/shard_map/ppermute | solution.py:29
  205.2 8.6 %collective-permute-start.29 = (f32[2,8,1,4,64]{4,1,3,2,0:T(8,128)S(1)}, f32[2,8,1,4,64]{4,1,3,2,0:T(8,128)S(1)}, u32[]{:S(2)}, u32[]{:S(2)}) collective-permute-start(f32[2,8,1,4,64]{4,1,3,2,0:T(8,128)S(1)} %get-tuple-element.50), channel_id=1, source_target_pairs={{0,1},{1,2},{2,3},{3,4},{4,5},{5,6},{6,7},{7,8},{8,9},{9,10},{10,1... | collective-permute-start | bytes 49160 | tf_op jit(solution)/shard_map/ppermute | solution.py:28
  227.3 9.9 %collective-permute-start.30 = (f32[2,8,1,8,128]{4,3,2,1,0:T(8,128)S(1)}, f32[2,8,1,8,128]{4,3,2,1,0:T(8,128)S(1)}, u32[]{:S(2)}, u32[]{:S(2)}) collective-permute-start(f32[2,8,1,8,128]{4,3,2,1,0:T(8,128)S(1)} %get-tuple-element.25), channel_id=1, source_target_pairs={{1,0},{2,1},{3,2},{4,3},{5,4},{6,5},{7,6},{8,7},{9,8},{10,9},{11,1... | collective-permute-start | bytes 196616 | tf_op jit(solution)/shard_map/ppermute | solution.py:29
  229.2 8.9 %collective-permute-start.31 = (f32[2,8,1,8,128]{4,3,2,1,0:T(8,128)S(1)}, f32[2,8,1,8,128]{4,3,2,1,0:T(8,128)S(1)}, u32[]{:S(2)}, u32[]{:S(2)}) collective-permute-start(f32[2,8,1,8,128]{4,3,2,1,0:T(8,128)S(1)} %get-tuple-element.26), channel_id=1, source_target_pairs={{0,1},{1,2},{2,3},{3,4},{4,5},{5,6},{6,7},{7,8},{8,9},{9,10},{10,1... | collective-permute-start | bytes 196616 | tf_op jit(solution)/shard_map/ppermute | solution.py:28
  239.0 9.2 %collective-permute-start.32 = (f32[2,8,1,8,128]{4,3,2,1,0:T(8,128)S(1)}, f32[2,8,1,8,128]{4,3,2,1,0:T(8,128)S(1)}, u32[]{:S(2)}, u32[]{:S(2)}) collective-permute-start(f32[2,8,1,8,128]{4,3,2,1,0:T(8,128)S(1)} %get-tuple-element.23), channel_id=1, source_target_pairs={{1,0},{2,1},{3,2},{4,3},{5,4},{6,5},{7,6},{8,7},{9,8},{10,9},{11,1... | collective-permute-start | bytes 196616 | tf_op jit(solution)/shard_map/ppermute | solution.py:29
  244.5 8.9 %collective-permute-start.33 = (f32[2,8,1,8,128]{4,3,2,1,0:T(8,128)S(1)}, f32[2,8,1,8,128]{4,3,2,1,0:T(8,128)S(1)}, u32[]{:S(2)}, u32[]{:S(2)}) collective-permute-start(f32[2,8,1,8,128]{4,3,2,1,0:T(8,128)S(1)} %get-tuple-element.24), channel_id=1, source_target_pairs={{0,1},{1,2},{2,3},{3,4},{4,5},{5,6},{6,7},{7,8},{8,9},{9,10},{10,1... | collective-permute-start | bytes 196616 | tf_op jit(solution)/shard_map/ppermute | solution.py:28
  280.6 11.8 %all-to-all-start.2 = ((f32[4,1,32768]{2,1,0:T(1,128)}), f32[4,1,32768]{2,1,0:T(1,128)S(1)}, u32[]{:S(2)}, u32[]{:S(2)}) async-start(f32[4,1,32768]{2,1,0:T(1,128)} %reshape.2439), calls=%async_computation.2 | async-start | bytes 1048576 | tf_op jit(solution)/shard_map/all_to_all | solution.py:230
  (9 other events, 78.3 us)
where the time goes:
time: 341 us; the launch traced here: 335 us
  waiting for transfers between devices  114 us (33%)
  local copies, waits for them, and re-layouts  90.2 us (26%)
  starting transfers between devices  88.6 us (26%)
  other arithmetic  28.5 us (8%)
  blocking collectives  10.5 us (3%)
    ppermute x17, waiting for transfers between devices, extended(): before = lax.ppermute(last, axis, up)  92.4 us
    ppermute x17, starting transfers between devices, extended(): before = lax.ppermute(last, axis, up)  40.8 us
    ppermute x17, starting transfers between devices, extended(): after = lax.ppermute(initial, axis, down)  36.3 us
    unnamed x10, local copies, waits for them, and re-layouts  33 us
    reshape x3, local copies, waits for them, and re-layouts, prolong_cells(): expanded.reshape(leading + (2 * first_extent, 2 * second_extent, 2 * thir...  11.5 us
    all_to_all x3, local copies, waits for them, and re-layouts, on_device(): lax.all_to_all(flattened, 'tm', split_axis=2, concat_axis=1, tiled=True)  11 us
    reduce_sum x8, other arithmetic, restrict_to_coarse(): jnp.mean(blocks, axis=(lead_count + 1, lead_count + 3, lead_count + 5))  10.8 us
    all_to_all x1, blocking collectives, on_device(): lax.all_to_all(values, 'tm', split_axis=0, concat_axis=1, tiled=True)  10.5 us
  transfers between devices with their start and end apart: 37, of which 20 were waited for; matrix products, arithmetic and copies ran while one was open for 5% of the time, Pallas kernels for 0%

commit v1 on v0

v1 whole, which is shorter than its diff:
```python
import math

import jax
import jax.numpy as jnp
import numpy as np
from jax import lax
from jax.experimental import pallas as pl
from jax.experimental.pallas import tpu as pltpu
from jax.sharding import PartitionSpec as P

MESH = pl.DeviceIdType.MESH
F32 = jnp.float32

ALPHA_CORNER = 0.01
STEP_SIZE = 0.5
DIFFUSE = 2.0
ADVECT = (0.2, -0.15, 0.1)
OMEGA = 0.7
KEEP = 1.0 - OMEGA
LENGTH = 64
BETA = ALPHA_CORNER ** (1.0 / LENGTH)

TM = 4
SLOTS = 8
LAYERS = 8
H0 = 3
H1 = 4
REACH = 8
N0 = LAYERS + 2 * H0
N1 = LAYERS // 2 + 2 * H1
N2 = LAYERS // 4 * (1 + 2 * REACH)
N3 = N2 // 2 - 2
SHIFTS = [d for k in range(1, REACH + 1) for d in (k, -k)]

FREQUENCIES = [[0, 8, 16, 24, 4, 12, 20, 28]] + [[k + 8 * m for m in range(8)] for k in (1, 2, 3)]


def shift_tables():
    table = np.zeros((TM, 32, 8, 128), np.float64)
    for a in range(TM):
        one, two, three = [], [], []
        for slot in range(SLOTS):
            phase = 2.0 * math.pi * FREQUENCIES[a][slot] / LENGTH
            first = (1.0 - BETA * math.cos(phase)) / STEP_SIZE
            second = BETA * math.sin(phase) / STEP_SIZE
            third = first
            if a == 0 and slot == 0:
                second, third = 0.0, (1.0 + BETA) / STEP_SIZE
            one.append(first)
            two.append(second)
            three.append(third)
        for slot in range(SLOTS):
            for c, values in enumerate((one, two, three)):
                table[a, 3 * slot + c] = values[slot]
                q, sb, lb = slot // 4, slot // 2 % 2, slot % 2
                table[a, 24 + 3 * q + c, 4 * sb : 4 * sb + 4, 64 * lb : 64 * lb + 64] = values[slot]
            lanes = slice(64 * q + 32 * lb, 64 * q + 32 * lb + 32)
            table[a, 30, 2 * sb : 2 * sb + 2, lanes] = one[slot]
            table[a, 30, 4 + 2 * sb : 6 + 2 * sb, lanes] = three[slot]
            table[a, 31, 2 * sb : 2 * sb + 2, lanes] = -two[slot]
            table[a, 31, 4 + 2 * sb : 6 + 2 * sb, lanes] = two[slot]
    return table.astype(np.float32)


def plus(a, b):
    return b if a is None else a if b is None else a + b


def minus(a, b):
    return a if b is None else -b if a is None else a - b


def scaled(a, factor):
    if a is None or abs(factor) < 1e-15:
        return None
    if abs(factor - 1.0) < 1e-15:
        return a
    if abs(factor + 1.0) < 1e-15:
        return -a
    return a * np.float32(factor)


def twisted(value, phase):
    c, s = math.cos(phase), math.sin(phase)
    re, im = value
    return (minus(scaled(re, c), scaled(im, s)), plus(scaled(re, s), scaled(im, c)))


def transform(values, sign):
    n = len(values)
    if n == 1:
        return values
    even = transform(values[0::2], sign)
    odd = transform(values[1::2], sign)
    upper, lower = [], []
    for k in range(n // 2):
        turned = twisted(odd[k], sign * 2.0 * math.pi * k / n)
        upper.append((plus(even[k][0], turned[0]), plus(even[k][1], turned[1])))
        lower.append((minus(even[k][0], turned[0]), minus(even[k][1], turned[1])))
    return upper + lower


def rows_lanes():
    return (
        lax.broadcasted_iota(jnp.int32, (8, 128), 0),
        lax.broadcasted_iota(jnp.int32, (8, 128), 1),
    )


class Level:
    def __init__(self, level, ny, nz, step=1):
        row, lane = rows_lanes()
        self.spread = DIFFUSE / 4.0**level
        bx, by, bz = (b / 2.0**level for b in ADVECT)
        c = self.spread
        self.xp, self.xm = np.float32(-c + bx), np.float32(-c - bx)
        self.step = step
        self.ny = ny
        zero = jnp.zeros((8, 128), F32)
        y, z = row % 8 % max(ny, 1), lane % nz
        if ny > 1:
            self.yp = jnp.where(y < ny - 1, np.float32(-c + by), zero)
            self.ym = jnp.where(y > 0, np.float32(-c - by), zero)
        self.zp = jnp.where(z < nz - step, np.float32(-c + bz), zero)
        self.zm = jnp.where(z >= step, np.float32(-c - bz), zero)

    def neighbours(self, below, here, above):
        total = self.xp * above + self.xm * below
        total += self.zp * pltpu.roll(here, 128 - self.step, 1)
        total += self.zm * pltpu.roll(here, self.step, 1)
        if self.ny > 1:
            total += self.yp * pltpu.roll(here, 7, 0)
            total += self.ym * pltpu.roll(here, 1, 0)
        return total


def block_sum(value):
    value = value + pltpu.roll(value, 7, 0)
    return value + pltpu.roll(value, 127, 1)


def block_sum_spread(value):
    row, lane = rows_lanes()
    value = value + jnp.where(row % 2 == 0, pltpu.roll(value, 7, 0), pltpu.roll(value, 1, 0))
    return value + jnp.where(lane % 2 == 0, pltpu.roll(value, 127, 1), pltpu.roll(value, 1, 1))


def take(value, index, axis):
    return jnp.take_along_axis(value, index, axis=axis, mode="promise_in_bounds")


def pack(tiles):
    row, lane = rows_lanes()
    even_lane, even_row = lane * 2 % 128, row * 2 % 8
    halves = []
    for left, right in tiles:
        if left is right:
            halves.append(take(left, even_lane, 1))
        else:
            halves.append(jnp.where(lane < 64, take(left, even_lane, 1), take(right, even_lane, 1)))
    if tiles[0] is tiles[1]:
        return take(halves[0], even_row, 0)
    return jnp.where(row < 4, take(halves[0], even_row, 0), take(halves[1], even_row, 0))


def unpack(tile, rb, lb):
    row, lane = rows_lanes()
    return take(take(tile, 4 * rb + row // 2, 0), 64 * lb + lane // 2, 1)


def layer_of(a, l):
    return 2 * a + l + (a // 2) * (1 - 2 * l)


def kernel(
    slabs,
    res,
    cap,
    tab_in,
    out,
    tab,
    series,
    spec,
    g0,
    v0,
    c0,
    d0,
    small0,
    g1,
    v1,
    c1,
    d1,
    g2,
    w2,
    v2,
    c2,
    d2,
    d3,
    solved,
    back,
    values,
    local_sem,
    a_send,
    a_recv,
    h_send,
    h_recv,
    k_send,
    k_recv,
):
    me, my = lax.axis_index("tm"), lax.axis_index("space")

    def peer(d):
        return lax.rem(me + d, TM)

    def slab(d):
        return lax.rem(my + (d + 8 * slabs), slabs)

    barrier = pltpu.get_barrier_semaphore()
    greeted = 0
    for d in range(1, TM):
        pl.semaphore_signal(barrier, inc=1, device_id=(peer(d), my), device_id_type=MESH)
        greeted += 1
    for d in SHIFTS:
        if d % slabs:
            pl.semaphore_signal(barrier, inc=1, device_id=(me, slab(d)), device_id_type=MESH)
            greeted += 1
    pl.semaphore_wait(barrier, greeted)

    sends = []

    def remote(src, dst, send, recv, device):
        copy = pltpu.make_async_remote_copy(
            src_ref=src,
            dst_ref=dst,
            send_sem=send,
            recv_sem=recv,
            device_id=device,
            device_id_type=MESH,
        )
        copy.start()
        sends.append(copy)
        return copy

    def across(src, dst, d, send, recv):
        if d % slabs:
            copy = remote(src, dst, send, recv, (me, slab(d)))
            return copy.wait_recv
        copy = pltpu.make_async_copy(src, dst, recv)
        copy.start()
        return copy.wait

    def exchange(phase, l, source, target, own):
        waits = []
        for d in (2, 1, 3):
            n = (phase * 2 + l) * 3 + d - 1
            copy = remote(source(peer(d)), target, a_send.at[n], a_recv.at[n], (peer(d), my))
            waits.append(copy.wait_recv)
        if own is not None:
            waits.append(own())
        return waits

    def local(src, dst, n):
        copy = pltpu.make_async_copy(src, dst, local_sem.at[n])
        copy.start()
        return copy.wait

    arrive = []
    for l in range(2):
        mine = series.at[pl.ds(16 * me, 16), l]
        arrive.append(
            exchange(
                0,
                l,
                lambda j, l=l: res.at[:, layer_of(j, l)],
                mine,
                lambda l=l, mine=mine: local(res.at[:, layer_of(me, l)], mine, l),
            )
        )
    table_wait = local(tab_in.at[me], tab, 2)

    n_cap = 0
    cap_waits = []

    def spread_cap(src, dst, d):
        nonlocal n_cap
        cap_waits.append(across(src, dst, d, k_send.at[n_cap], k_recv.at[n_cap]))
        n_cap += 1

    spread_cap(cap.at[pl.ds(0, H0)], c0.at[pl.ds(H0 + LAYERS, H0)], -1)
    spread_cap(cap.at[pl.ds(LAYERS - H0, H0)], c0.at[pl.ds(0, H0)], 1)
    for i in range(LAYERS):
        c0[H0 + i] = cap[i]
    for i in range(LAYERS // 2):
        tile = block_sum(cap[2 * i] + cap[2 * i + 1]) * np.float32(0.125)
        c1[H1 + i] = pack(((tile, tile),) * 2)
    spread_cap(c1.at[pl.ds(H1, 4)], c1.at[pl.ds(H1 + 4, 4)], -1)
    spread_cap(c1.at[pl.ds(H1, 4)], c1.at[pl.ds(0, 4)], 1)
    for i in range(LAYERS // 4):
        tile = block_sum(c1[H1 + 2 * i] + c1[H1 + 2 * i + 1]) * np.float32(0.125)
        c2[2 * REACH + i] = pack(((tile, tile),) * 2)
    for d in SHIFTS:
        spread_cap(c2.at[pl.ds(2 * REACH, 2)], c2.at[pl.ds(2 * (REACH - d), 2)], d)

    table_wait()
    for wait in cap_waits:
        wait()

    def weight(index, extent):
        inside = jnp.logical_and(index >= 0, index < extent)
        return jnp.where(inside, np.float32(OMEGA), np.float32(0.0))

    six = [np.float32(6.0 * DIFFUSE / 4.0**level) for level in range(4)]

    def invert(c, first, second, third, diagonal, w):
        top, q, bottom = c * first + diagonal, c * second, c * third + diagonal
        scale = w / (top * bottom + q * q)
        return bottom * scale, q * scale, top * scale

    def invert0(slot, carry):
        first, second, third = (tab[3 * slot + k] for k in range(3))
        for i in range(N0):
            w = weight(LAYERS * my + i - H0, LAYERS * slabs)
            parts = invert(c0[i], first, second, third, six[0], w)
            for k in range(3):
                d0[slot, k, i] = parts[k]
        return carry

    lax.fori_loop(0, SLOTS, invert0, 0)
    for q in range(2):
        first, second, third = (tab[24 + 3 * q + k] for k in range(3))
        for i in range(N1):
            w = weight(4 * my + i - H1, 4 * slabs)
            parts = invert(c1[i], first, second, third, six[1], w)
            for k in range(3):
                d1[q, k, i] = parts[k]

    same, swapped = tab[30], tab[31]

    def diagonal(c, level):
        return c * same + six[level], c * swapped

    def swap(value):
        return pltpu.roll(value, 4, 0)

    def invert_packed(c, level, w):
        a, b = diagonal(c, level)
        other = swap(a)
        scale = w / (a * other + b * b)
        return other * scale, -b * scale

    for i in range(N2):
        parts = invert_packed(c2[i], 2, weight(2 * my + i - 2 * REACH, 2 * slabs))
        d2[0, i], d2[1, i] = parts
    for i in range(N3):
        c = block_sum_spread(c2[2 * i + 2] + c2[2 * i + 3]) * np.float32(0.125)
        parts = invert_packed(c, 3, weight(my + i - (REACH - 1), slabs))
        d3[0, i], d3[1, i] = parts

    def forward(l):
        middle = [[None] * 8 for _ in range(5)]
        for t2 in range(8):
            column = [
                (series[8 * t1 + t2, l] * np.float32(BETA ** (8 * t1 + t2)), None)
                for t1 in range(8)
            ]
            first = transform(column, -1.0)
            for k1 in range(5):
                middle[k1][t2] = twisted(first[k1], -2.0 * math.pi * k1 * t2 / LENGTH)
        for k1 in range(5):
            last = transform(middle[k1], -1.0)
            if k1 == 0:
                spec[0, 0, 0, l], spec[0, 1, 0, l] = last[0][0], last[4][0]
                chosen = [(m, 0, m) for m in (1, 2, 3)]
            elif k1 == 4:
                chosen = [(m, 0, 4 + m) for m in range(4)]
            else:
                chosen = [(m, k1, m) for m in range(8)]
            for m, j, slot in chosen:
                spec[j, 0, slot, l], spec[j, 1, slot, l] = last[m]

    solve = []
    for l in range(2):
        for wait in arrive[l]:
            wait()
        forward(l)
        solve.append(
            exchange(
                1,
                l,
                lambda j, l=l: spec.at[j, :, :, l],
                g0.at[:, :, H0 + layer_of(me, l)],
                None,
            )
        )
        here = H0 + layer_of(me, l)
        for c in range(2):
            for slot in range(SLOTS):
                g0[c, slot, here] = spec[me, c, slot, l]

    n_halo = 0
    halo_waits = []

    def spread_halo(src, dst, d):
        nonlocal n_halo
        halo_waits.append(across(src, dst, d, h_send.at[n_halo], h_recv.at[n_halo]))
        n_halo += 1

    for l in range(2):
        for wait in solve[l]:
            wait()
        for a in range(TM):
            x = layer_of(a, l)
            if x < H0:
                spread_halo(g0.at[:, :, H0 + x], g0.at[:, :, H0 + LAYERS + x], -1)
            if x >= LAYERS - H0:
                spread_halo(g0.at[:, :, H0 + x], g0.at[:, :, x - (LAYERS - H0)], 1)
    for wait in halo_waits:
        wait()
    halo_waits.clear()

    def jacobi(inverse, er, ei):
        a, b, c = inverse
        return a * er + b * ei, c * ei - b * er

    def sweep(level, below, here, above, g, inverse):
        er = g[0] - level.neighbours(below[0], here[0], above[0])
        ei = g[1] - level.neighbours(below[1], here[1], above[1])
        ur, ui = jacobi(inverse, er, ei)
        keep = np.float32(KEEP)
        return keep * here[0] + ur, keep * here[1] + ui

    def defect(level, below, here, above, g, c, shifts, six_here):
        first, second, third = shifts
        q = c * second
        er = g[0] - level.neighbours(below[0], here[0], above[0])
        ei = g[1] - level.neighbours(below[1], here[1], above[1])
        er = er - ((c * first + six_here) * here[0] - q * here[1])
        ei = ei - (q * here[0] + (c * third + six_here) * here[1])
        return er, ei

    def pre(level, count, own, load_g, load_d, load_c, shifts, six_here, keep_v, keep_r):
        once, twice, waiting = {}, {}, None
        for i in range(count):
            once[i] = jacobi(load_d(i), *load_g(i))
            if i < 2:
                continue
            j = i - 1
            twice[j] = sweep(level, once[j - 1], once[j], once[j + 1], load_g(j), load_d(j))
            keep_v(j, twice[j])
            j = i - 2
            if j - own[0] in range(own[1]):
                r = defect(
                    level,
                    twice[j - 1],
                    twice[j],
                    twice[j + 1],
                    load_g(j),
                    load_c(j),
                    shifts,
                    six_here,
                )
                if (j - own[0]) % 2:
                    keep_r((j - own[0]) // 2, (waiting[0] + r[0], waiting[1] + r[1]))
                waiting = r

    def post(level, first, count, load_v, load_g, load_d, keep):
        once = {}
        start = {}
        for i in range(first - 2, first + count + 2):
            start[i] = load_v(i)
            j = i - 1
            if j < first - 1:
                continue
            once[j] = sweep(level, start[j - 1], start[j], start[j + 1], load_g(j), load_d(j))
            j = i - 2
            if j < first:
                continue
            keep(j, sweep(level, once[j - 1], once[j], once[j + 1], load_g(j), load_d(j)))

    eighth = np.float32(0.125)
    level0 = Level(0, 8, 128)
    level1 = Level(1, 4, 64)
    level2 = Level(2, 2, 32)
    level3 = Level(3, 1, 32, 2)

    def down0(slot, carry):
        def keep_v(i, v):
            v0[slot, 0, i], v0[slot, 1, i] = v

        def keep_r(i, r):
            for c in range(2):
                small0[slot, c, i] = block_sum(r[c]) * eighth

        pre(
            level0,
            N0,
            (H0, LAYERS),
            lambda i: (g0[0, slot, i], g0[1, slot, i]),
            lambda i: tuple(d0[slot, k, i] for k in range(3)),
            lambda i: c0[i],
            tuple(tab[3 * slot + k] for k in range(3)),
            six[0],
            keep_v,
            keep_r,
        )
        return carry

    lax.fori_loop(0, SLOTS, down0, 0)

    for q in range(2):
        for c in range(2):
            for i in range(4):
                tiles = [[small0[4 * q + 2 * sb + lb, c, i] for lb in range(2)] for sb in range(2)]
                g1[q, c, H1 + i] = pack(tiles)
    spread_halo(g1.at[:, :, pl.ds(H1, 4)], g1.at[:, :, pl.ds(H1 + 4, 4)], -1)
    spread_halo(g1.at[:, :, pl.ds(H1, 4)], g1.at[:, :, pl.ds(0, 4)], 1)
    for wait in halo_waits:
        wait()
    halo_waits.clear()

    coarse = {}
    for q in range(2):

        def keep_v(i, v, q=q):
            v1[q, 0, i], v1[q, 1, i] = v

        def keep_r(i, r, q=q):
            for c in range(2):
                coarse[q, c, i] = block_sum(r[c]) * eighth

        pre(
            level1,
            N1,
            (H1, 4),
            lambda i, q=q: (g1[q, 0, i], g1[q, 1, i]),
            lambda i, q=q: tuple(d1[q, k, i] for k in range(3)),
            lambda i: c1[i],
            tuple(tab[24 + 3 * q + k] for k in range(3)),
            six[1],
            keep_v,
            keep_r,
        )
    for i in range(2):
        g2[2 * REACH + i] = pack([[coarse[q, c, i] for q in range(2)] for c in range(2)])
    for d in SHIFTS:
        spread_halo(g2.at[pl.ds(2 * REACH, 2)], g2.at[pl.ds(2 * (REACH - d), 2)], d)
    for wait in halo_waits:
        wait()
    halo_waits.clear()

    def relax(d, i, e):
        return d[0, i] * e + d[1, i] * swap(e)

    def sweep_packed(level, below, here, above, g, d, i):
        return np.float32(KEEP) * here + relax(d, i, g - level.neighbours(below, here, above))

    for i in range(N2):
        w2[i] = relax(d2, i, g2[i])
    for i in range(1, N2 - 1):
        v2[i] = sweep_packed(level2, w2[i - 1], w2[i], w2[i + 1], g2[i], d2, i)
    right = []
    for m in range(N3):
        pair = []
        for i in (2 * m + 2, 2 * m + 3):
            here = v2[i]
            a, b = diagonal(c2[i], 2)
            pair.append(
                g2[i]
                - level2.neighbours(v2[i - 1], here, v2[i + 1])
                - (a * here + b * swap(here))
            )
        right.append(block_sum_spread(pair[0] + pair[1]) * eighth)
    current = {m: relax(d3, m, right[m]) for m in range(N3)}
    for s in range(1, 6):
        current = {
            m: sweep_packed(
                level3, current[m - 1], current[m], current[m + 1], right[m], d3, m
            )
            for m in range(s, N3 - s)
        }
    low = 2 * 5 + 2
    stage = {i: v2[i] + current[(i - 2) // 2] for i in range(low, low + 10)}
    for s in range(1, 3):
        stage = {
            i: sweep_packed(level2, stage[i - 1], stage[i], stage[i + 1], g2[i], d2, i)
            for i in range(low + s, low + 10 - s)
        }

    for q in range(2):
        correction = {}

        def load_v(i, q=q, correction=correction):
            m = 2 * REACH + (i - H1) // 2
            if m not in correction:
                correction[m] = [unpack(stage[m], c, q) for c in range(2)]
            return tuple(v1[q, c, i] + correction[m][c] for c in range(2))

        def keep(i, v, q=q):
            v1[q, 0, i], v1[q, 1, i] = v

        post(
            level1,
            H1 - 1,
            6,
            load_v,
            lambda i, q=q: (g1[q, 0, i], g1[q, 1, i]),
            lambda i, q=q: tuple(d1[q, k, i] for k in range(3)),
            keep,
        )

    def up0(slot, carry):
        q, sb, lb = slot // 4, slot // 2 % 2, slot % 2
        correction = {}

        def load_v(i):
            m = H1 + (i - H0) // 2
            if m not in correction:
                correction[m] = [unpack(v1[q, c, m], sb, lb) for c in range(2)]
            return tuple(v0[slot, c, i] + correction[m][c] for c in range(2))

        def keep(i, v):
            solved[0, slot, i - H0], solved[1, slot, i - H0] = v

        post(
            level0,
            H0,
            LAYERS,
            load_v,
            lambda i: (g0[0, slot, i], g0[1, slot, i]),
            lambda i: tuple(d0[slot, k, i] for k in range(3)),
            keep,
        )
        return carry

    lax.fori_loop(0, SLOTS, up0, 0)

    arrive = []
    for l in range(2):
        arrive.append(
            exchange(
                2, l, lambda j, l=l: solved.at[:, :, layer_of(j, l)], back.at[me, :, :, l], None
            )
        )
        for c in range(2):
            for slot in range(SLOTS):
                back[me, c, slot, l] = solved[c, slot, layer_of(me, l)]

    def inverse(l):
        def field(j, slot, factor=2.0):
            return tuple(back[j, c, slot, l] * np.float32(factor) for c in range(2))

        nothing = (None, None)
        packed = field(0, 0, 1.0)
        line = [(packed[0], None)] + [field(0, m) for m in (1, 2, 3)] + [(packed[1], None)]
        line = transform(line + [nothing] * 3, 1.0)
        middle = [[(line[t2][0], None) for t2 in range(8)]]
        for k1 in (1, 2, 3):
            line = transform([field(k1, m) for m in range(8)], 1.0)
            middle.append(
                [twisted(line[t2], 2.0 * math.pi * k1 * t2 / LENGTH) for t2 in range(8)]
            )
        line = transform([field(0, 4 + m) for m in range(4)] + [nothing] * 4, 1.0)
        turned = [twisted(line[t2], 2.0 * math.pi * 4 * t2 / LENGTH) for t2 in range(8)]
        middle.append([(turned[t2][0], None) for t2 in range(8)])
        for t2 in range(8):
            column = transform([middle[k1][t2] for k1 in range(5)] + [nothing] * 3, 1.0)
            for t1 in range(8):
                t = 8 * t1 + t2
                values[l, t] = column[t1][0] * np.float32(BETA ** (-t) / LENGTH)

    finish = []
    for l in range(2):
        for wait in arrive[l]:
            wait()
        inverse(l)
        mine = out.at[:, layer_of(me, l)]
        finish += exchange(
            3,
            l,
            lambda j, l=l: values.at[l, pl.ds(16 * j, 16)],
            mine,
            lambda l=l, mine=mine: local(values.at[l, pl.ds(16 * me, 16)], mine, 3 + l),
        )
    for wait in finish:
        wait()
    for copy in sends:
        copy.wait_send()


def solution(mesh):
    slabs = mesh.shape["space"]
    table = shift_tables()

    def tiles(*lead):
        return pltpu.VMEM(lead + (8, 128), F32)

    def on_device(residual, capacity):
        any_space = pl.BlockSpec(memory_space=pl.ANY)
        dma = pltpu.SemaphoreType.DMA
        return pl.pallas_call(
            lambda *refs: kernel(slabs, *refs),
            out_shape=jax.ShapeDtypeStruct(residual.shape, F32),
            in_specs=[any_space, pl.BlockSpec(memory_space=pltpu.VMEM), any_space],
            out_specs=any_space,
            scratch_shapes=[
                tiles(32),
                tiles(LENGTH, 2),
                tiles(TM, 2, SLOTS, 2),
                tiles(2, SLOTS, N0),
                tiles(SLOTS, 2, N0),
                tiles(N0),
                tiles(SLOTS, 3, N0),
                tiles(SLOTS, 2, 4),
                tiles(2, 2, N1),
                tiles(2, 2, N1),
                tiles(N1),
                tiles(2, 3, N1),
                tiles(N2),
                tiles(N2),
                tiles(N2),
                tiles(N2),
                tiles(2, N2),
                tiles(2, N3),
                tiles(2, SLOTS, LAYERS),
                tiles(TM, 2, SLOTS, 2),
                tiles(2, LENGTH),
                dma((5,)),
                dma((24,)),
                dma((24,)),
                dma((24,)),
                dma((24,)),
                dma((20,)),
                dma((20,)),
            ],
            compiler_params=pltpu.CompilerParams(collective_id=0, has_side_effects=True),
            name="paradiag",
        )(residual, capacity, jnp.asarray(table))

    return jax.shard_map(
        on_device,
        mesh=mesh,
        in_specs=(P("tm", "space", None, None), P("space", None, None)),
        out_specs=P("tm", "space", None, None),
        check_vma=False,
    )
```

time: 341 us -> 59.9 us (0.18)
  the two profiles are of different devices: /device:TPU:128 before, /device:TPU:16 now
where the time goes in v1:
time: 59.9 us; the launch traced here: 59.3 us
  Pallas kernels  57.4 us (96%)
  local copies, waits for them, and re-layouts  1.89 us (3%)
    pallas_call x1, Pallas kernels, on_device(): pl.pallas_call(lambda *refs: kernel(slabs, *refs), out_shape=jax.ShapeDty...  57.4 us
    unnamed x1, local copies, waits for them, and re-layouts  1.89 us

profile of v1, /device:TPU:16, one launch (start us, length us, event | category | flops | bytes accessed | tf_op | source)
XLA Modules:
  0.0 59.3 jit_solution(11332994827490304173)
XLA Ops:
  0.0 57.4 %paradiag.1 = f32[16,8,8,128]{3,2,1,0:T(8,128)} custom-call(f32[16,8,8,128]{3,2,1,0:T(8,128)} %refs_0_.1, f32[8,8,128]{2,1,0:T(8,128)} %refs_1_.1, f32[4,32,8,128]{3,2,1,0:T(8,128)} %constant.2.clone.refs_2_), custom_call_target="tpu_custom_call" | custom-call | tf_op jit(solution)/shard_map/paradiag/pallas_call | solution.py:700
  57.4 1.9 %copy.5 = f32[16,8,8,128]{3,2,1,0:T(8,128)} copy(f32[16,8,8,128]{3,2,1,0:T(8,128)} %paradiag.1) | data formatting | bytes 1048576

commit v2 on v1

--- a/solution.py
+++ b/solution.py
@@ -30,13 +30,13 @@
 N1 = LAYERS // 2 + 2 * H1
 N2 = LAYERS // 4 * (1 + 2 * REACH)
 N3 = N2 // 2 - 2
-SHIFTS = [d for k in range(1, REACH + 1) for d in (k, -k)]
+SHIFTS = [d for k in (4, 5, 3, 6, 2, 7, 8, 1) for d in (k, -k)]
 
 FREQUENCIES = [[0, 8, 16, 24, 4, 12, 20, 28]] + [[k + 8 * m for m in range(8)] for k in (1, 2, 3)]
 
 
 def shift_tables():
-    table = np.zeros((TM, 32, 8, 128), np.float64)
+    table = np.zeros((TM, 34, 8, 128), np.float64)
     for a in range(TM):
         one, two, three = [], [], []
         for slot in range(SLOTS):
@@ -54,11 +54,11 @@
                 table[a, 3 * slot + c] = values[slot]
                 q, sb, lb = slot // 4, slot // 2 % 2, slot % 2
                 table[a, 24 + 3 * q + c, 4 * sb : 4 * sb + 4, 64 * lb : 64 * lb + 64] = values[slot]
-            lanes = slice(64 * q + 32 * lb, 64 * q + 32 * lb + 32)
-            table[a, 30, 2 * sb : 2 * sb + 2, lanes] = one[slot]
-            table[a, 30, 4 + 2 * sb : 6 + 2 * sb, lanes] = three[slot]
-            table[a, 31, 2 * sb : 2 * sb + 2, lanes] = -two[slot]
-            table[a, 31, 4 + 2 * sb : 6 + 2 * sb, lanes] = two[slot]
+            for lanes in (slice(32 * lb, 32 * lb + 32), slice(64 + 32 * lb, 96 + 32 * lb)):
+                table[a, 30 + 2 * q, 2 * sb : 2 * sb + 2, lanes] = one[slot]
+                table[a, 30 + 2 * q, 4 + 2 * sb : 6 + 2 * sb, lanes] = three[slot]
+                table[a, 31 + 2 * q, 2 * sb : 2 * sb + 2, lanes] = -two[slot]
+                table[a, 31 + 2 * q, 4 + 2 * sb : 6 + 2 * sb, lanes] = two[slot]
     return table.astype(np.float32)
 
 
@@ -174,10 +174,12 @@
 
 def kernel(
     slabs,
+    res_in,
+    cap_in,
+    tab_in,
+    out,
     res,
     cap,
-    tab_in,
-    out,
     tab,
     series,
     spec,
@@ -215,6 +217,15 @@
     def slab(d):
         return lax.rem(my + (d + 8 * slabs), slabs)
 
+    def local(src, dst, n):
+        copy = pltpu.make_async_copy(src, dst, local_sem.at[n])
+        copy.start()
+        return copy.wait
+
+    res_wait = local(res_in, res, 0)
+    cap_wait = local(cap_in, cap, 1)
+    table_wait = local(tab_in.at[me], tab, 2)
+
     barrier = pltpu.get_barrier_semaphore()
     greeted = 0
     for d in range(1, TM):
@@ -249,35 +260,29 @@
         copy.start()
         return copy.wait
 
-    def exchange(phase, l, source, target, own):
+    def exchange(first, source, target):
         waits = []
         for d in (2, 1, 3):
-            n = (phase * 2 + l) * 3 + d - 1
+            n = first + d - 1
             copy = remote(source(peer(d)), target, a_send.at[n], a_recv.at[n], (peer(d), my))
             waits.append(copy.wait_recv)
-        if own is not None:
-            waits.append(own())
         return waits
 
-    def local(src, dst, n):
-        copy = pltpu.make_async_copy(src, dst, local_sem.at[n])
-        copy.start()
-        return copy.wait
-
+    res_wait()
     arrive = []
     for l in range(2):
-        mine = series.at[pl.ds(16 * me, 16), l]
         arrive.append(
             exchange(
-                0,
-                l,
+                3 * l,
                 lambda j, l=l: res.at[:, layer_of(j, l)],
-                mine,
-                lambda l=l, mine=mine: local(res.at[:, layer_of(me, l)], mine, l),
+                series.at[pl.ds(16 * me, 16), l],
             )
         )
-    table_wait = local(tab_in.at[me], tab, 2)
-
+    for l in range(2):
+        for t in range(16):
+            series[16 * me + t, l] = res[t, layer_of(me, l)]
+
+    cap_wait()
     n_cap = 0
     cap_waits = []
 
@@ -300,61 +305,6 @@
         c2[2 * REACH + i] = pack(((tile, tile),) * 2)
     for d in SHIFTS:
         spread_cap(c2.at[pl.ds(2 * REACH, 2)], c2.at[pl.ds(2 * (REACH - d), 2)], d)
-
-    table_wait()
-    for wait in cap_waits:
-        wait()
-
-    def weight(index, extent):
-        inside = jnp.logical_and(index >= 0, index < extent)
-        return jnp.where(inside, np.float32(OMEGA), np.float32(0.0))
-
-    six = [np.float32(6.0 * DIFFUSE / 4.0**level) for level in range(4)]
-
-    def invert(c, first, second, third, diagonal, w):
-        top, q, bottom = c * first + diagonal, c * second, c * third + diagonal
-        scale = w / (top * bottom + q * q)
-        return bottom * scale, q * scale, top * scale
-
-    def invert0(slot, carry):
-        first, second, third = (tab[3 * slot + k] for k in range(3))
-        for i in range(N0):
-            w = weight(LAYERS * my + i - H0, LAYERS * slabs)
-            parts = invert(c0[i], first, second, third, six[0], w)
-            for k in range(3):
-                d0[slot, k, i] = parts[k]
-        return carry
-
-    lax.fori_loop(0, SLOTS, invert0, 0)
-    for q in range(2):
-        first, second, third = (tab[24 + 3 * q + k] for k in range(3))
-        for i in range(N1):
-            w = weight(4 * my + i - H1, 4 * slabs)
-            parts = invert(c1[i], first, second, third, six[1], w)
-            for k in range(3):
-                d1[q, k, i] = parts[k]
-
-    same, swapped = tab[30], tab[31]
-
-    def diagonal(c, level):
-        return c * same + six[level], c * swapped
-
-    def swap(value):
-        return pltpu.roll(value, 4, 0)
-
-    def invert_packed(c, level, w):
-        a, b = diagonal(c, level)
-        other = swap(a)
-        scale = w / (a * other + b * b)
-        return other * scale, -b * scale
-
-    for i in range(N2):
-        parts = invert_packed(c2[i], 2, weight(2 * my + i - 2 * REACH, 2 * slabs))
-        d2[0, i], d2[1, i] = parts
-    for i in range(N3):
-        c = block_sum_spread(c2[2 * i + 2] + c2[2 * i + 3]) * np.float32(0.125)
-        parts = invert_packed(c, 3, weight(my + i - (REACH - 1), slabs))
-        d3[0, i], d3[1, i] = parts
 
     def forward(l):
         middle = [[None] * 8 for _ in range(5)]
@@ -378,45 +328,100 @@
             for m, j, slot in chosen:
                 spec[j, 0, slot, l], spec[j, 1, slot, l] = last[m]
 
-    solve = []
+    solve = {}
     for l in range(2):
         for wait in arrive[l]:
             wait()
         forward(l)
-        solve.append(
-            exchange(
-                1,
-                l,
-                lambda j, l=l: spec.at[j, :, :, l],
-                g0.at[:, :, H0 + layer_of(me, l)],
-                None,
+        for q in range(2):
+            four = pl.ds(4 * q, 4)
+            solve[l, q] = exchange(
+                6 + 6 * l + 3 * q,
+                lambda j, l=l, four=four: spec.at[j, :, four, l],
+                g0.at[:, four, H0 + layer_of(me, l)],
             )
-        )
         here = H0 + layer_of(me, l)
         for c in range(2):
             for slot in range(SLOTS):
                 g0[c, slot, here] = spec[me, c, slot, l]
 
+    table_wait()
+    for wait in cap_waits:
+        wait()
+
+    def weight(index, extent):
+        inside = jnp.logical_and(index >= 0, index < extent)
+        return jnp.where(inside, np.float32(OMEGA), np.float32(0.0))
+
+    six = [np.float32(6.0 * DIFFUSE / 4.0**level) for level in range(4)]
+
+    def invert(c, first, second, third, diagonal, w):
+        top, q, bottom = c * first + diagonal, c * second, c * third + diagonal
+        scale = w / (top * bottom + q * q)
+        return bottom * scale, q * scale, top * scale
+
+    def invert0(slot, carry):
+        first, second, third = (tab[3 * slot + k] for k in range(3))
+        for i in range(N0):
+            w = weight(LAYERS * my + i - H0, LAYERS * slabs)
+            parts = invert(c0[i], first, second, third, six[0], w)
+            for k in range(3):
+                d0[slot, k, i] = parts[k]
+        return carry
+
+    lax.fori_loop(0, SLOTS, invert0, 0)
+    for q in range(2):
+        first, second, third = (tab[24 + 3 * q + k] for k in range(3))
+        for i in range(N1):
+            w = weight(4 * my + i - H1, 4 * slabs)
+            parts = invert(c1[i], first, second, third, six[1], w)
+            for k in range(3):
+                d1[q, k, i] = parts[k]
+
+    def diagonal(c, q, level):
+        return c * tab[30 + 2 * q] + six[level], c * tab[31 + 2 * q]
+
+    def swap(value):
+        return pltpu.roll(value, 4, 0)
+
+    def invert_packed(c, q, level, w):
+        a, b = diagonal(c, q, level)
+        other = swap(a)
+        scale = w / (a * other + b * b)
+        return other * scale, -b * scale
+
+    for i in range(N2):
+        w = weight(2 * my + i - 2 * REACH, 2 * slabs)
+        for q in range(2):
+            parts = invert_packed(c2[i], q, 2, w)
+            d2[q, 0, i], d2[q, 1, i] = parts
+    for i in range(N3):
+        c = block_sum_spread(c2[2 * i + 2] + c2[2 * i + 3]) * np.float32(0.125)
+        w = weight(my + i - (REACH - 1), slabs)
+        for q in range(2):
+            parts = invert_packed(c, q, 3, w)
+            d3[q, 0, i], d3[q, 1, i] = parts
+
     n_halo = 0
-    halo_waits = []
-
-    def spread_halo(src, dst, d):
+
+    def spread(src, dst, d):
         nonlocal n_halo
-        halo_waits.append(across(src, dst, d, h_send.at[n_halo], h_recv.at[n_halo]))
         n_halo += 1
-
+        return across(src, dst, d, h_send.at[n_halo - 1], h_recv.at[n_halo - 1])
+
+    halo = {0: [], 1: []}
     for l in range(2):
-        for wait in solve[l]:
-            wait()
-        for a in range(TM):
-            x = layer_of(a, l)
-            if x < H0:
-                spread_halo(g0.at[:, :, H0 + x], g0.at[:, :, H0 + LAYERS + x], -1)
-            if x >= LAYERS - H0:
-                spread_halo(g0.at[:, :, H0 + x], g0.at[:, :, x - (LAYERS - H0)], 1)
-    for wait in halo_waits:
-        wait()
-    halo_waits.clear()
+        for q in range(2):
+            for wait in solve[l, q]:
+                wait()
+            four = pl.ds(4 * q, 4)
+            for a in range(TM):
+                x = layer_of(a, l)
+                here = g0.at[:, four, H0 + x]
+                if x < H0:
+                    halo[q].append(spread(here, g0.at[:, four, H0 + LAYERS + x], -1))
+                if x >= LAYERS - H0:
+                    halo[q].append(spread(here, g0.at[:, four, x - (LAYERS - H0)], 1))
 
     def jacobi(inverse, er, ei):
         a, b, c = inverse
@@ -505,28 +510,31 @@
         )
         return carry
 
-    lax.fori_loop(0, SLOTS, down0, 0)
-
     for q in range(2):
+        for wait in halo[q]:
+            wait()
+        lax.fori_loop(4 * q, 4 * q + 4, down0, 0)
         for c in range(2):
             for i in range(4):
                 tiles = [[small0[4 * q + 2 * sb + lb, c, i] for lb in range(2)] for sb in range(2)]
                 g1[q, c, H1 + i] = pack(tiles)
-    spread_halo(g1.at[:, :, pl.ds(H1, 4)], g1.at[:, :, pl.ds(H1 + 4, 4)], -1)
-    spread_halo(g1.at[:, :, pl.ds(H1, 4)], g1.at[:, :, pl.ds(0, 4)], 1)
-    for wait in halo_waits:
-        wait()
-    halo_waits.clear()
-
-    coarse = {}
+        mine = g1.at[q, :, pl.ds(H1, 4)]
+        halo[q] = [
+            spread(mine, g1.at[q, :, pl.ds(H1 + 4, 4)], -1),
+            spread(mine, g1.at[q, :, pl.ds(0, 4)], 1),
+        ]
+
     for q in range(2):
+        for wait in halo[q]:
+            wait()
+        coarse = {}
 
         def keep_v(i, v, q=q):
             v1[q, 0, i], v1[q, 1, i] = v
 
-        def keep_r(i, r, q=q):
+        def keep_r(i, r, coarse=coarse):
             for c in range(2):
-                coarse[q, c, i] = block_sum(r[c]) * eighth
+                coarse[c, i] = block_sum(r[c]) * eighth
 
         pre(
             level1,
@@ -540,62 +548,63 @@
             keep_v,
             keep_r,
         )
-    for i in range(2):
-        g2[2 * REACH + i] = pack([[coarse[q, c, i] for q in range(2)] for c in range(2)])
-    for d in SHIFTS:
-        spread_halo(g2.at[pl.ds(2 * REACH, 2)], g2.at[pl.ds(2 * (REACH - d), 2)], d)
-    for wait in halo_waits:
-        wait()
-    halo_waits.clear()
-
-    def relax(d, i, e):
-        return d[0, i] * e + d[1, i] * swap(e)
-
-    def sweep_packed(level, below, here, above, g, d, i):
-        return np.float32(KEEP) * here + relax(d, i, g - level.neighbours(below, here, above))
-
-    for i in range(N2):
-        w2[i] = relax(d2, i, g2[i])
-    for i in range(1, N2 - 1):
-        v2[i] = sweep_packed(level2, w2[i - 1], w2[i], w2[i + 1], g2[i], d2, i)
-    right = []
-    for m in range(N3):
-        pair = []
-        for i in (2 * m + 2, 2 * m + 3):
-            here = v2[i]
-            a, b = diagonal(c2[i], 2)
-            pair.append(
-                g2[i]
-                - level2.neighbours(v2[i - 1], here, v2[i + 1])
-                - (a * here + b * swap(here))
-            )
-        right.append(block_sum_spread(pair[0] + pair[1]) * eighth)
-    current = {m: relax(d3, m, right[m]) for m in range(N3)}
-    for s in range(1, 6):
-        current = {
-            m: sweep_packed(
-                level3, current[m - 1], current[m], current[m + 1], right[m], d3, m
-            )
-            for m in range(s, N3 - s)
-        }
-    low = 2 * 5 + 2
-    stage = {i: v2[i] + current[(i - 2) // 2] for i in range(low, low + 10)}
-    for s in range(1, 3):
-        stage = {
-            i: sweep_packed(level2, stage[i - 1], stage[i], stage[i + 1], g2[i], d2, i)
-            for i in range(low + s, low + 10 - s)
-        }
-
-    for q in range(2):
+        for i in range(2):
+            g2[q, 2 * REACH + i] = pack([[coarse[c, i], coarse[c, i]] for c in range(2)])
+        halo[q] = [
+            spread(g2.at[q, pl.ds(2 * REACH, 2)], g2.at[q, pl.ds(2 * (REACH - d), 2)], d)
+            for d in SHIFTS
+        ]
+
+    def relax(d, q, i, e):
+        return d[q, 0, i] * e + d[q, 1, i] * swap(e)
+
+    def sweep_packed(level, below, here, above, g, d, q, i):
+        return np.float32(KEEP) * here + relax(d, q, i, g - level.neighbours(below, here, above))
+
+    def coarse_levels(q):
+        for i in range(N2):
+            w2[i] = relax(d2, q, i, g2[q, i])
+        for i in range(1, N2 - 1):
+            v2[i] = sweep_packed(level2, w2[i - 1], w2[i], w2[i + 1], g2[q, i], d2, q, i)
+        right = []
+        for m in range(N3):
+            pair = []
+            for i in (2 * m + 2, 2 * m + 3):
+                here = v2[i]
+                a, b = diagonal(c2[i], q, 2)
+                pair.append(
+                    g2[q, i]
+                    - level2.neighbours(v2[i - 1], here, v2[i + 1])
+                    - (a * here + b * swap(here))
+                )
+            right.append(block_sum_spread(pair[0] + pair[1]) * eighth)
+        current = {m: relax(d3, q, m, right[m]) for m in range(N3)}
+        for s in range(1, 6):
+            current = {
+                m: sweep_packed(
+                    level3, current[m - 1], current[m], current[m + 1], right[m], d3, q, m
+                )
+                for m in range(s, N3 - s)
+            }
+        low = 2 * 5 + 2
+        stage = {i: v2[i] + current[(i - 2) // 2] for i in range(low, low + 10)}
+        for s in range(1, 3):
+            stage = {
+                i: sweep_packed(level2, stage[i - 1], stage[i], stage[i + 1], g2[q, i], d2, q, i)
+                for i in range(low + s, low + 10 - s)
+            }
+        return stage
+
+    def up1(q, stage):
         correction = {}
 
-        def load_v(i, q=q, correction=correction):
+        def load_v(i):
             m = 2 * REACH + (i - H1) // 2
             if m not in correction:
-                correction[m] = [unpack(stage[m], c, q) for c in range(2)]
+                correction[m] = [unpack(stage[m], c, 0) for c in range(2)]
             return tuple(v1[q, c, i] + correction[m][c] for c in range(2))
 
-        def keep(i, v, q=q):
+        def keep(i, v):
             v1[q, 0, i], v1[q, 1, i] = v
 
         post(
@@ -603,8 +612,8 @@
             H1 - 1,
             6,
             load_v,
-            lambda i, q=q: (g1[q, 0, i], g1[q, 1, i]),
-            lambda i, q=q: tuple(d1[q, k, i] for k in range(3)),
+            lambda i: (g1[q, 0, i], g1[q, 1, i]),
+            lambda i: tuple(d1[q, k, i] for k in range(3)),
             keep,
         )
 
@@ -632,18 +641,24 @@
         )
         return carry
 
-    lax.fori_loop(0, SLOTS, up0, 0)
-
-    arrive = []
-    for l in range(2):
-        arrive.append(
-            exchange(
-                2, l, lambda j, l=l: solved.at[:, :, layer_of(j, l)], back.at[me, :, :, l], None
+    arrive = [[], []]
+    for q in range(2):
+        for wait in halo[q]:
+            wait()
+        stage = coarse_levels(q)
+        up1(q, stage)
+        lax.fori_loop(4 * q, 4 * q + 4, up0, 0)
+        four = pl.ds(4 * q, 4)
+        for l in range(2):
+            arrive[l] += exchange(
+                18 + 6 * q + 3 * l,
+                lambda j, l=l, four=four: solved.at[:, four, layer_of(j, l)],
+                back.at[me, :, four, l],
             )
-        )
-        for c in range(2):
-            for slot in range(SLOTS):
-                back[me, c, slot, l] = solved[c, slot, layer_of(me, l)]
+        for l in range(2):
+            for c in range(2):
+                for slot in range(4 * q, 4 * q + 4):
+                    back[me, c, slot, l] = solved[c, slot, layer_of(me, l)]
 
     def inverse(l):
         def field(j, slot, factor=2.0):
@@ -674,13 +689,8 @@
             wait()
         inverse(l)
         mine = out.at[:, layer_of(me, l)]
-        finish += exchange(
-            3,
-            l,
-            lambda j, l=l: values.at[l, pl.ds(16 * j, 16)],
-            mine,
-            lambda l=l, mine=mine: local(values.at[l, pl.ds(16 * me, 16)], mine, 3 + l),
-        )
+        finish += exchange(30 + 3 * l, lambda j, l=l: values.at[l, pl.ds(16 * j, 16)], mine)
+        finish.append(local(values.at[l, pl.ds(16 * me, 16)], mine, 3 + l))
     for wait in finish:
         wait()
     for copy in sends:
@@ -700,10 +710,12 @@
         return pl.pallas_call(
             lambda *refs: kernel(slabs, *refs),
             out_shape=jax.ShapeDtypeStruct(residual.shape, F32),
-            in_specs=[any_space, pl.BlockSpec(memory_space=pltpu.VMEM), any_space],
+            in_specs=[any_space] * 3,
             out_specs=any_space,
             scratch_shapes=[
-                tiles(32),
+                tiles(16, LAYERS),
+                tiles(LAYERS),
+                tiles(34),
                 tiles(LENGTH, 2),
                 tiles(TM, 2, SLOTS, 2),
                 tiles(2, SLOTS, N0),
@@ -715,20 +727,20 @@
                 tiles(2, 2, N1),
                 tiles(N1),
                 tiles(2, 3, N1),
+                tiles(2, N2),
                 tiles(N2),
                 tiles(N2),
                 tiles(N2),
-                tiles(N2),
-                tiles(2, N2),
-                tiles(2, N3),
+                tiles(2, 2, N2),
+                tiles(2, 2, N3),
                 tiles(2, SLOTS, LAYERS),
                 tiles(TM, 2, SLOTS, 2),
                 tiles(2, LENGTH),
                 dma((5,)),
-                dma((24,)),
-                dma((24,)),
-                dma((24,)),
-                dma((24,)),
+                dma((36,)),
+                dma((36,)),
+                dma((48,)),
+                dma((48,)),
                 dma((20,)),
                 dma((20,)),
             ],

time: 59.9 us -> 55.8 us (0.932)
  Pallas kernels: 57.4 us -> 53.8 us
    pallas_call x1, Pallas kernels: 57.4 us -> 53.8 us  [on_device(): pl.pallas_call(lambda *refs: kernel(slabs, *refs), out_shape=jax.ShapeDty...]
where the time goes in v2:
time: 55.8 us; the launch traced here: 55.6 us
  Pallas kernels  53.8 us (96%)
  local copies, waits for them, and re-layouts  1.89 us (3%)
    pallas_call x1, Pallas kernels, on_device(): pl.pallas_call(lambda *refs: kernel(slabs, *refs), out_shape=jax.ShapeDty...  53.8 us
    unnamed x1, local copies, waits for them, and re-layouts  1.89 us

profile of v2, /device:TPU:16, one launch (start us, length us, event | category | flops | bytes accessed | tf_op | source)
XLA Modules:
  0.0 55.6 jit_solution(15519511539986801180)
XLA Ops:
  0.0 53.8 %paradiag.1 = f32[16,8,8,128]{3,2,1,0:T(8,128)} custom-call(f32[16,8,8,128]{3,2,1,0:T(8,128)} %refs_0_.1, f32[8,8,128]{2,1,0:T(8,128)} %refs_1_.1, f32[4,34,8,128]{3,2,1,0:T(8,128)} %constant.2.clone.refs_2_), custom_call_target="tpu_custom_call" | custom-call | tf_op jit(solution)/shard_map/paradiag/pallas_call | solution.py:710
  53.8 1.9 %copy.5 = f32[16,8,8,128]{3,2,1,0:T(8,128)} copy(f32[16,8,8,128]{3,2,1,0:T(8,128)} %paradiag.1) | data formatting | bytes 1048576

commit v3 on v2

--- a/solution.py
+++ b/solution.py
@@ -201,13 +201,10 @@
     solved,
     back,
     values,
+    p2,
     local_sem,
-    a_send,
-    a_recv,
-    h_send,
-    h_recv,
-    k_send,
-    k_recv,
+    send_sem,
+    recv_sem,
 ):
     me, my = lax.axis_index("tm"), lax.axis_index("space")
 
@@ -237,59 +234,42 @@
             greeted += 1
     pl.semaphore_wait(barrier, greeted)
 
-    sends = []
-
-    def remote(src, dst, send, recv, device):
-        copy = pltpu.make_async_remote_copy(
+    def remote(src, dst, out_sem, in_sem, device):
+        pltpu.make_async_remote_copy(
             src_ref=src,
             dst_ref=dst,
-            send_sem=send,
-            recv_sem=recv,
+            send_sem=send_sem.at[out_sem],
+            recv_sem=recv_sem.at[in_sem],
             device_id=device,
             device_id_type=MESH,
-        )
-        copy.start()
-        sends.append(copy)
-        return copy
-
-    def across(src, dst, d, send, recv):
-        if d % slabs:
-            copy = remote(src, dst, send, recv, (me, slab(d)))
-            return copy.wait_recv
-        copy = pltpu.make_async_copy(src, dst, recv)
-        copy.start()
-        return copy.wait
-
-    def exchange(first, source, target):
-        waits = []
+        ).start()
+
+    def landed(size, n):
+        pltpu.make_async_copy(size, size, recv_sem.at[n]).wait()
+
+    def sent(size, n):
+        pltpu.make_async_copy(size, size, send_sem.at[n]).wait()
+
+    def exchange(out_sem, in_sem, source, target):
         for d in (2, 1, 3):
-            n = first + d - 1
-            copy = remote(source(peer(d)), target, a_send.at[n], a_recv.at[n], (peer(d), my))
-            waits.append(copy.wait_recv)
-        return waits
+            remote(source(peer(d)), target, out_sem, in_sem, (peer(d), my))
 
     res_wait()
-    arrive = []
     for l in range(2):
-        arrive.append(
-            exchange(
-                3 * l,
-                lambda j, l=l: res.at[:, layer_of(j, l)],
-                series.at[pl.ds(16 * me, 16), l],
-            )
+        exchange(
+            0,
+            0 + l,
+            lambda j, l=l: res.at[:, layer_of(j, l)],
+            series.at[pl.ds(16 * me, 16), l],
         )
     for l in range(2):
         for t in range(16):
             series[16 * me + t, l] = res[t, layer_of(me, l)]
 
     cap_wait()
-    n_cap = 0
-    cap_waits = []
 
     def spread_cap(src, dst, d):
-        nonlocal n_cap
-        cap_waits.append(across(src, dst, d, k_send.at[n_cap], k_recv.at[n_cap]))
-        n_cap += 1
+        remote(src, dst, 7, 15, (me, slab(d)))
 
     spread_cap(cap.at[pl.ds(0, H0)], c0.at[pl.ds(H0 + LAYERS, H0)], -1)
     spread_cap(cap.at[pl.ds(LAYERS - H0, H0)], c0.at[pl.ds(0, H0)], 1)
@@ -328,15 +308,14 @@
             for m, j, slot in chosen:
                 spec[j, 0, slot, l], spec[j, 1, slot, l] = last[m]
 
-    solve = {}
     for l in range(2):
-        for wait in arrive[l]:
-            wait()
+        landed(series.at[pl.ds(0, 48), l], l)
         forward(l)
         for q in range(2):
             four = pl.ds(4 * q, 4)
-            solve[l, q] = exchange(
-                6 + 6 * l + 3 * q,
+            exchange(
+                1,
+                2 + 2 * l + q,
                 lambda j, l=l, four=four: spec.at[j, :, four, l],
                 g0.at[:, four, H0 + layer_of(me, l)],
             )
@@ -346,8 +325,7 @@
                 g0[c, slot, here] = spec[me, c, slot, l]
 
     table_wait()
-    for wait in cap_waits:
-        wait()
+    landed(series.at[pl.ds(0, 46), 0], 15)
 
     def weight(index, extent):
         inside = jnp.logical_and(index >= 0, index < extent)
@@ -402,26 +380,20 @@
             parts = invert_packed(c, q, 3, w)
             d3[q, 0, i], d3[q, 1, i] = parts
 
-    n_halo = 0
-
-    def spread(src, dst, d):
-        nonlocal n_halo
-        n_halo += 1
-        return across(src, dst, d, h_send.at[n_halo - 1], h_recv.at[n_halo - 1])
-
-    halo = {0: [], 1: []}
+    def spread(src, dst, d, out_sem, in_sem):
+        remote(src, dst, out_sem, in_sem, (me, slab(d)))
+
     for l in range(2):
         for q in range(2):
-            for wait in solve[l, q]:
-                wait()
             four = pl.ds(4 * q, 4)
+            landed(spec.at[pl.ds(0, 3), :, four, l], 2 + 2 * l + q)
             for a in range(TM):
                 x = layer_of(a, l)
                 here = g0.at[:, four, H0 + x]
                 if x < H0:
-                    halo[q].append(spread(here, g0.at[:, four, H0 + LAYERS + x], -1))
+                    spread(here, g0.at[:, four, H0 + LAYERS + x], -1, 4, 9 + q)
                 if x >= LAYERS - H0:
-                    halo[q].append(spread(here, g0.at[:, four, x - (LAYERS - H0)], 1))
+                    spread(here, g0.at[:, four, x - (LAYERS - H0)], 1, 4, 9 + q)
 
     def jacobi(inverse, er, ei):
         a, b, c = inverse
@@ -511,22 +483,18 @@
         return carry
 
     for q in range(2):
-        for wait in halo[q]:
-            wait()
+        landed(g0.at[:, pl.ds(4 * q, 4), pl.ds(0, 2 * H0)], 9 + q)
         lax.fori_loop(4 * q, 4 * q + 4, down0, 0)
         for c in range(2):
             for i in range(4):
                 tiles = [[small0[4 * q + 2 * sb + lb, c, i] for lb in range(2)] for sb in range(2)]
                 g1[q, c, H1 + i] = pack(tiles)
         mine = g1.at[q, :, pl.ds(H1, 4)]
-        halo[q] = [
-            spread(mine, g1.at[q, :, pl.ds(H1 + 4, 4)], -1),
-            spread(mine, g1.at[q, :, pl.ds(0, 4)], 1),
-        ]
+        spread(mine, g1.at[q, :, pl.ds(H1 + 4, 4)], -1, 5, 11 + q)
+        spread(mine, g1.at[q, :, pl.ds(0, 4)], 1, 5, 11 + q)
 
     for q in range(2):
-        for wait in halo[q]:
-            wait()
+        landed(g1.at[q, :, pl.ds(0, 8)], 11 + q)
         coarse = {}
 
         def keep_v(i, v, q=q):
@@ -548,12 +516,9 @@
             keep_v,
             keep_r,
         )
-        for i in range(2):
-            g2[q, 2 * REACH + i] = pack([[coarse[c, i], coarse[c, i]] for c in range(2)])
-        halo[q] = [
-            spread(g2.at[q, pl.ds(2 * REACH, 2)], g2.at[q, pl.ds(2 * (REACH - d), 2)], d)
-            for d in SHIFTS
-        ]
+        p2[q, REACH] = pack([[coarse[c, 0], coarse[c, 1]] for c in range(2)])
+        for d in SHIFTS:
+            spread(p2.at[q, REACH], p2.at[q, REACH - d], d, 6, 13 + q)
 
     def relax(d, q, i, e):
         return d[q, 0, i] * e + d[q, 1, i] * swap(e)
@@ -562,6 +527,8 @@
         return np.float32(KEEP) * here + relax(d, q, i, g - level.neighbours(below, here, above))
 
     def coarse_levels(q):
+        for i in range(N2 // 2):
+            g2[q, 2 * i], g2[q, 2 * i + 1] = p2[q, i], pltpu.roll(p2[q, i], 64, 1)
         for i in range(N2):
             w2[i] = relax(d2, q, i, g2[q, i])
         for i in range(1, N2 - 1):
@@ -617,8 +584,8 @@
             keep,
         )
 
-    def up0(slot, carry):
-        q, sb, lb = slot // 4, slot // 2 % 2, slot % 2
+    def up0(q, k, carry):
+        slot, sb, lb = 4 * q + k, k >> 1, k & 1
         correction = {}
 
         def load_v(i):
@@ -641,17 +608,16 @@
         )
         return carry
 
-    arrive = [[], []]
     for q in range(2):
-        for wait in halo[q]:
-            wait()
+        landed(p2.at[q, pl.ds(0, 2 * REACH)], 13 + q)
         stage = coarse_levels(q)
         up1(q, stage)
-        lax.fori_loop(4 * q, 4 * q + 4, up0, 0)
+        lax.fori_loop(0, 4, lambda k, carry, q=q: up0(q, k, carry), 0)
         four = pl.ds(4 * q, 4)
         for l in range(2):
-            arrive[l] += exchange(
-                18 + 6 * q + 3 * l,
+            exchange(
+                2,
+                6 + l,
                 lambda j, l=l, four=four: solved.at[:, four, layer_of(j, l)],
                 back.at[me, :, four, l],
             )
@@ -683,18 +649,28 @@
                 t = 8 * t1 + t2
                 values[l, t] = column[t1][0] * np.float32(BETA ** (-t) / LENGTH)
 
-    finish = []
     for l in range(2):
-        for wait in arrive[l]:
-            wait()
+        landed(back.at[pl.ds(0, 3), :, :, l], 6 + l)
         inverse(l)
         mine = out.at[:, layer_of(me, l)]
-        finish += exchange(30 + 3 * l, lambda j, l=l: values.at[l, pl.ds(16 * j, 16)], mine)
-        finish.append(local(values.at[l, pl.ds(16 * me, 16)], mine, 3 + l))
-    for wait in finish:
-        wait()
-    for copy in sends:
-        copy.wait_send()
+        exchange(3, 8, lambda j, l=l: values.at[l, pl.ds(16 * j, 16)], mine)
+        for t in range(16):
+            out[t, layer_of(me, l)] = values[l, 16 * me + t]
+    sent(series.at[pl.ds(0, 48)], 0)
+    sent(spec.at[pl.ds(0, 3)], 1)
+    sent(back.at[pl.ds(0, 3)], 2)
+    sent(g0.at[:, :, pl.ds(0, 2 * H0)], 4)
+    sent(g1.at[:, :, pl.ds(0, 8)], 5)
+    sent(p2.at[:, pl.ds(0, 2 * REACH)], 6)
+    sent(series.at[pl.ds(0, 46), 0], 7)
+    sent(values.at[:, pl.ds(0, 48)], 3)
+    landed(values.at[:, pl.ds(0, 48)], 8)
+
+
+def write_out(src, dst, sem):
+    copy = pltpu.make_async_copy(src, dst, sem.at[0])
+    copy.start()
+    copy.wait()
 
 
 def solution(mesh):
@@ -707,11 +683,11 @@
     def on_device(residual, capacity):
         any_space = pl.BlockSpec(memory_space=pl.ANY)
         dma = pltpu.SemaphoreType.DMA
-        return pl.pallas_call(
+        result = pl.pallas_call(
             lambda *refs: kernel(slabs, *refs),
             out_shape=jax.ShapeDtypeStruct(residual.shape, F32),
             in_specs=[any_space] * 3,
-            out_specs=any_space,
+            out_specs=pl.BlockSpec(memory_space=pltpu.VMEM),
             scratch_shapes=[
                 tiles(16, LAYERS),
                 tiles(LAYERS),
@@ -736,17 +712,23 @@
                 tiles(2, SLOTS, LAYERS),
                 tiles(TM, 2, SLOTS, 2),
                 tiles(2, LENGTH),
-                dma((5,)),
-                dma((36,)),
-                dma((36,)),
-                dma((48,)),
-                dma((48,)),
-                dma((20,)),
-                dma((20,)),
+                tiles(2, 1 + 2 * REACH),
+                dma((3,)),
+                dma((8,)),
+                dma((16,)),
             ],
-            compiler_params=pltpu.CompilerParams(collective_id=0, has_side_effects=True),
+            compiler_params=pltpu.CompilerParams(collective_id=0, has_side_effects=True, vmem_limit_bytes=24 << 20),
             name="paradiag",
-        )(residual, capacity, jnp.asarray(table))
+        )(*(pltpu.with_memory_space_constraint(v, pltpu.HBM) for v in (residual, capacity, jnp.asarray(table))))
+        return pl.pallas_call(
+            write_out,
+            out_shape=jax.ShapeDtypeStruct(residual.shape, F32),
+            in_specs=[pl.BlockSpec(memory_space=pltpu.VMEM)],
+            out_specs=any_space,
+            scratch_shapes=[dma((1,))],
+            compiler_params=pltpu.CompilerParams(vmem_limit_bytes=1 << 20),
+            name="write_out",
+        )(result)
 
     return jax.shard_map(
         on_device,

time: 55.8 us -> 52.7 us (0.944)
  local copies, waits for them, and re-layouts: 1.89 us -> 0 us
  Pallas kernels: 53.8 us -> 52.6 us
    pallas_call x1, Pallas kernels: 53.8 us -> 51.8 us  [on_device(): pl.pallas_call(lambda *refs: kernel(slabs, *refs), out_shape=jax.ShapeDty...]
    unnamed x1 -> x0, local copies, waits for them, and re-layouts: 1.89 us -> none
    pallas_call x0 -> x1, Pallas kernels: none -> 0.8 us  [on_device(): pl.pallas_call(write_out, out_shape=jax.ShapeDtypeStruct(residual.shape,...]
where the time goes in v3:
time: 52.7 us; the launch traced here: 52.6 us
  Pallas kernels  52.6 us (100%)
    pallas_call x1, Pallas kernels, on_device(): pl.pallas_call(lambda *refs: kernel(slabs, *refs), out_shape=jax.ShapeDty...  51.8 us

profile of v3, /device:TPU:16, one launch (start us, length us, event | category | flops | bytes accessed | tf_op | source)
XLA Modules:
  0.0 52.6 jit_solution(8298230230026780417)
XLA Ops:
  0.0 51.8 %paradiag.1.src = f32[16,8,8,128]{3,2,1,0:T(8,128)S(1)} custom-call(f32[16,8,8,128]{3,2,1,0:T(8,128)} %refs_0_.1, f32[8,8,128]{2,1,0:T(8,128)} %refs_1_.1, f32[4,34,8,128]{3,2,1,0:T(8,128)} %constant.2.clone.refs_2_), custom_call_target="tpu_custom_call" | custom-call | tf_op jit(solution)/shard_map/paradiag/pallas_call | solution.py:686
  51.8 0.8 %write_out.1 = f32[16,8,8,128]{3,2,1,0:T(8,128)} custom-call(f32[16,8,8,128]{3,2,1,0:T(8,128)S(1)} %paradiag.1.src), custom_call_target="tpu_custom_call" | custom-call | tf_op jit(solution)/shard_map/write_out/pallas_call | solution.py:723

commit v4 on v3

--- a/solution.py
+++ b/solution.py
@@ -202,6 +202,7 @@
     back,
     values,
     p2,
+    o0,
     local_sem,
     send_sem,
     recv_sem,
@@ -460,31 +461,79 @@
     level2 = Level(2, 2, 32)
     level3 = Level(3, 1, 32, 2)
 
-    def down0(slot, carry):
-        def keep_v(i, v):
-            v0[slot, 0, i], v0[slot, 1, i] = v
-
-        def keep_r(i, r):
-            for c in range(2):
-                small0[slot, c, i] = block_sum(r[c]) * eighth
-
-        pre(
-            level0,
-            N0,
-            (H0, LAYERS),
+    def looped(start, count, together, body):
+        def some(n, carry):
+            for k in range(together):
+                body(start + n * together + k, carry)
+            return carry
+
+        if together == count:
+            some(0, 0)
+        else:
+            lax.fori_loop(0, count // together, some, 0)
+
+    def views0(slot):
+        return (
             lambda i: (g0[0, slot, i], g0[1, slot, i]),
             lambda i: tuple(d0[slot, k, i] for k in range(3)),
-            lambda i: c0[i],
-            tuple(tab[3 * slot + k] for k in range(3)),
-            six[0],
-            keep_v,
-            keep_r,
         )
+
+    def keep0(slot, i, v):
+        v0[slot, 0, i], v0[slot, 1, i] = v
+
+    def coarsen0(slot, twice, layers, load_g):
+        shifts = tuple(tab[3 * slot + k] for k in range(3))
+        for i in layers:
+            pair = [
+                defect(
+                    level0, twice[j - 1], twice[j], twice[j + 1], load_g(j), c0[j], shifts, six[0]
+                )
+                for j in (i, i + 1)
+            ]
+            for c in range(2):
+                small0[slot, c, (i - H0) // 2] = block_sum(pair[0][c] + pair[1][c]) * eighth
+
+    first, last = H0, H0 + LAYERS - 1
+
+    def inside0(slot, carry):
+        load_g, load_d = views0(slot)
+        once, twice = {}, {}
+        for i in range(first, last + 1):
+            once[i] = jacobi(load_d(i), *load_g(i))
+            if i - 2 >= first:
+                j = i - 1
+                twice[j] = sweep(level0, once[j - 1], once[j], once[j + 1], load_g(j), load_d(j))
+                keep0(slot, j, twice[j])
+        for n, i in enumerate((first, first + 1, last - 1, last)):
+            o0[slot, 0, n], o0[slot, 1, n] = once[i]
+        coarsen0(slot, twice, range(first + 2, last - 2, 2), load_g)
         return carry
+
+    def outside0(slot, carry):
+        load_g, load_d = views0(slot)
+        for edge, step, stored in ((first, -1, (0, 1)), (last, 1, (3, 2))):
+            once = {
+                edge: (o0[slot, 0, stored[0]], o0[slot, 1, stored[0]]),
+                edge - step: (o0[slot, 0, stored[1]], o0[slot, 1, stored[1]]),
+            }
+            twice = {
+                i: (v0[slot, 0, i], v0[slot, 1, i]) for i in (edge - step, edge - 2 * step)
+            }
+            for n in range(1, H0 + 1):
+                i = edge + n * step
+                once[i] = jacobi(load_d(i), *load_g(i))
+                j = i - step
+                twice[j] = sweep(level0, once[j - 1], once[j], once[j + 1], load_g(j), load_d(j))
+                keep0(slot, j, twice[j])
+            coarsen0(slot, twice, (min(edge, edge - step),), load_g)
+        return carry
+
+    for q in range(2):
+        looped(4 * q, 4, 4, inside0)
 
     for q in range(2):
         landed(g0.at[:, pl.ds(4 * q, 4), pl.ds(0, 2 * H0)], 9 + q)
-        lax.fori_loop(4 * q, 4 * q + 4, down0, 0)
+        looped(4 * q, 4, 4, outside0)
         for c in range(2):
             for i in range(4):
                 tiles = [[small0[4 * q + 2 * sb + lb, c, i] for lb in range(2)] for sb in range(2)]
@@ -612,15 +661,16 @@
         landed(p2.at[q, pl.ds(0, 2 * REACH)], 13 + q)
         stage = coarse_levels(q)
         up1(q, stage)
-        lax.fori_loop(0, 4, lambda k, carry, q=q: up0(q, k, carry), 0)
-        four = pl.ds(4 * q, 4)
-        for l in range(2):
-            exchange(
-                2,
-                6 + l,
-                lambda j, l=l, four=four: solved.at[:, four, layer_of(j, l)],
-                back.at[me, :, four, l],
-            )
+        for k, size in ((0, 2), (2, 2)) if q == 0 else ((0, 4),):
+            looped(k, size, 2, lambda k, carry, q=q: up0(q, k, carry))
+            some = pl.ds(4 * q + k, size)
+            for l in range(2):
+                exchange(
+                    2,
+                    6 + l,
+                    lambda j, l=l, some=some: solved.at[:, some, layer_of(j, l)],
+                    back.at[me, :, some, l],
+                )
         for l in range(2):
             for c in range(2):
                 for slot in range(4 * q, 4 * q + 4):
@@ -713,6 +763,7 @@
                 tiles(TM, 2, SLOTS, 2),
                 tiles(2, LENGTH),
                 tiles(2, 1 + 2 * REACH),
+                tiles(SLOTS, 2, 4),
                 dma((3,)),
                 dma((8,)),
                 dma((16,)),

time: 52.7 us -> 51.1 us (0.970)
  Pallas kernels: 52.6 us -> 51 us
    pallas_call x1, Pallas kernels: 51.8 us -> 50.2 us  [on_device(): pl.pallas_call(lambda *refs: kernel(slabs, *refs), out_shape=jax.ShapeDty...]
where the time goes in v4:
time: 51.1 us; the launch traced here: 51 us
  Pallas kernels  51 us (100%)
    pallas_call x1, Pallas kernels, on_device(): pl.pallas_call(lambda *refs: kernel(slabs, *refs), out_shape=jax.ShapeDty...  50.2 us

profile of v4, /device:TPU:16, one launch (start us, length us, event | category | flops | bytes accessed | tf_op | source)
XLA Modules:
  0.0 51.0 jit_solution(1837658168088599196)
XLA Ops:
  0.0 50.2 %paradiag.1.src = f32[16,8,8,128]{3,2,1,0:T(8,128)S(1)} custom-call(f32[16,8,8,128]{3,2,1,0:T(8,128)} %refs_0_.1, f32[8,8,128]{2,1,0:T(8,128)} %refs_1_.1, f32[4,34,8,128]{3,2,1,0:T(8,128)} %constant.2.clone.refs_2_), custom_call_target="tpu_custom_call" | custom-call | tf_op jit(solution)/shard_map/paradiag/pallas_call | solution.py:736
  50.2 0.8 %write_out.1 = f32[16,8,8,128]{3,2,1,0:T(8,128)} custom-call(f32[16,8,8,128]{3,2,1,0:T(8,128)S(1)} %paradiag.1.src), custom_call_target="tpu_custom_call" | custom-call | tf_op jit(solution)/shard_map/write_out/pallas_call | solution.py:774

commit v5 on v4

--- a/solution.py
+++ b/solution.py
@@ -23,8 +23,9 @@
 TM = 4
 SLOTS = 8
 LAYERS = 8
-H0 = 3
+H0 = 6
 H1 = 4
+OWN1 = 2
 REACH = 8
 N0 = LAYERS + 2 * H0
 N1 = LAYERS // 2 + 2 * H1
@@ -326,7 +327,7 @@
                 g0[c, slot, here] = spec[me, c, slot, l]
 
     table_wait()
-    landed(series.at[pl.ds(0, 46), 0], 15)
+    landed(series.at[pl.ds(0, 52), 0], 15)
 
     def weight(index, extent):
         inside = jnp.logical_and(index >= 0, index < extent)
@@ -416,11 +417,11 @@
         ei = ei - (q * here[0] + (c * third + six_here) * here[1])
         return er, ei
 
-    def pre(level, count, own, load_g, load_d, load_c, shifts, six_here, keep_v, keep_r):
+    def pre(level, layers, own, load_g, load_d, load_c, shifts, six_here, keep_v, keep_r):
         once, twice, waiting = {}, {}, None
-        for i in range(count):
+        for i in layers:
             once[i] = jacobi(load_d(i), *load_g(i))
-            if i < 2:
+            if i < layers[2]:
                 continue
             j = i - 1
             twice[j] = sweep(level, once[j - 1], once[j], once[j + 1], load_g(j), load_d(j))
@@ -491,7 +492,7 @@
                 for j in (i, i + 1)
             ]
             for c in range(2):
-                small0[slot, c, (i - H0) // 2] = block_sum(pair[0][c] + pair[1][c]) * eighth
+                small0[slot, c, (i - H0) // 2 + OWN1] = block_sum(pair[0][c] + pair[1][c]) * eighth
 
     first, last = H0, H0 + LAYERS - 1
 
@@ -524,26 +525,38 @@
                 once[i] = jacobi(load_d(i), *load_g(i))
                 j = i - step
                 twice[j] = sweep(level0, once[j - 1], once[j], once[j + 1], load_g(j), load_d(j))
-                keep0(slot, j, twice[j])
-            coarsen0(slot, twice, (min(edge, edge - step),), load_g)
+                if n <= 3:
+                    keep0(slot, j, twice[j])
+            pairs = [min(edge - step, edge) + 2 * n * step for n in range(1 + OWN1)]
+            coarsen0(slot, twice, pairs, load_g)
         return carry
 
     for q in range(2):
         looped(4 * q, 4, 4, inside0)
 
+    def views1(q):
+        return (
+            lambda i: (g1[q, 0, i], g1[q, 1, i]),
+            lambda i: tuple(d1[q, k, i] for k in range(3)),
+        )
+
     for q in range(2):
         landed(g0.at[:, pl.ds(4 * q, 4), pl.ds(0, 2 * H0)], 9 + q)
-        looped(4 * q, 4, 4, outside0)
+        looped(4 * q, 4, 2, outside0)
         for c in range(2):
-            for i in range(4):
+            for i in range(4 + 2 * OWN1):
                 tiles = [[small0[4 * q + 2 * sb + lb, c, i] for lb in range(2)] for sb in range(2)]
-                g1[q, c, H1 + i] = pack(tiles)
-        mine = g1.at[q, :, pl.ds(H1, 4)]
-        spread(mine, g1.at[q, :, pl.ds(H1 + 4, 4)], -1, 5, 11 + q)
-        spread(mine, g1.at[q, :, pl.ds(0, 4)], 1, 5, 11 + q)
-
-    for q in range(2):
-        landed(g1.at[q, :, pl.ds(0, 8)], 11 + q)
+                g1[q, c, H1 - OWN1 + i] = pack(tiles)
+        far = H1 - OWN1
+        spread(g1.at[q, :, pl.ds(H1, far)], g1.at[q, :, pl.ds(0, far)], 1, 5, 11 + q)
+        spread(
+            g1.at[q, :, pl.ds(H1 + 4 - far, far)],
+            g1.at[q, :, pl.ds(N1 - far, far)],
+            -1,
+            5,
+            11 + q,
+        )
+
         coarse = {}
 
         def keep_v(i, v, q=q):
@@ -553,12 +566,13 @@
             for c in range(2):
                 coarse[c, i] = block_sum(r[c]) * eighth
 
+        load_g, load_d = views1(q)
         pre(
             level1,
-            N1,
+            range(H1 - OWN1, H1 + 4 + OWN1),
             (H1, 4),
-            lambda i, q=q: (g1[q, 0, i], g1[q, 1, i]),
-            lambda i, q=q: tuple(d1[q, k, i] for k in range(3)),
+            load_g,
+            load_d,
             lambda i: c1[i],
             tuple(tab[24 + 3 * q + k] for k in range(3)),
             six[1],
@@ -568,6 +582,15 @@
         p2[q, REACH] = pack([[coarse[c, 0], coarse[c, 1]] for c in range(2)])
         for d in SHIFTS:
             spread(p2.at[q, REACH], p2.at[q, REACH - d], d, 6, 13 + q)
+
+    for q in range(2):
+        landed(g1.at[q, :, pl.ds(0, 2 * (H1 - OWN1))], 11 + q)
+        load_g, load_d = views1(q)
+        for low in (0, N1 - 4):
+            once = {i: jacobi(load_d(i), *load_g(i)) for i in range(low, low + 4)}
+            for i in (low + 1, low + 2):
+                v = sweep(level1, once[i - 1], once[i], once[i + 1], load_g(i), load_d(i))
+                v1[q, 0, i], v1[q, 1, i] = v
 
     def relax(d, q, i, e):
         return d[q, 0, i] * e + d[q, 1, i] * swap(e)
@@ -628,8 +651,7 @@
             H1 - 1,
             6,
             load_v,
-            lambda i: (g1[q, 0, i], g1[q, 1, i]),
-            lambda i: tuple(d1[q, k, i] for k in range(3)),
+            *views1(q),
             keep,
         )
 
@@ -710,9 +732,9 @@
     sent(spec.at[pl.ds(0, 3)], 1)
     sent(back.at[pl.ds(0, 3)], 2)
     sent(g0.at[:, :, pl.ds(0, 2 * H0)], 4)
-    sent(g1.at[:, :, pl.ds(0, 8)], 5)
+    sent(g1.at[:, :, pl.ds(0, 2 * (H1 - OWN1))], 5)
     sent(p2.at[:, pl.ds(0, 2 * REACH)], 6)
-    sent(series.at[pl.ds(0, 46), 0], 7)
+    sent(series.at[pl.ds(0, 52), 0], 7)
     sent(values.at[:, pl.ds(0, 48)], 3)
     landed(values.at[:, pl.ds(0, 48)], 8)
 
@@ -748,7 +770,7 @@
                 tiles(SLOTS, 2, N0),
                 tiles(N0),
                 tiles(SLOTS, 3, N0),
-                tiles(SLOTS, 2, 4),
+                tiles(SLOTS, 2, 4 + 2 * OWN1),
                 tiles(2, 2, N1),
                 tiles(2, 2, N1),
                 tiles(N1),

time: 51.1 us -> 49.3 us (0.965); the launches traced: 51 us -> 48.3 us
  Pallas kernels: 51 us -> 48.3 us
    pallas_call x1, Pallas kernels: 50.2 us -> 47.5 us  [on_device(): pl.pallas_call(lambda *refs: kernel(slabs, *refs), out_shape=jax.ShapeDty...]
where the time goes in v5:
time: 49.3 us; the launch traced here: 48.3 us
  Pallas kernels  48.3 us (98%)
    pallas_call x1, Pallas kernels, on_device(): pl.pallas_call(lambda *refs: kernel(slabs, *refs), out_shape=jax.ShapeDty...  47.5 us

profile of v5, /device:TPU:16, one launch (start us, length us, event | category | flops | bytes accessed | tf_op | source)
XLA Modules:
  0.0 48.3 jit_solution(18226980737257596912)
XLA Ops:
  0.0 47.5 %paradiag.1.src = f32[16,8,8,128]{3,2,1,0:T(8,128)S(1)} custom-call(f32[16,8,8,128]{3,2,1,0:T(8,128)} %refs_0_.1, f32[8,8,128]{2,1,0:T(8,128)} %refs_1_.1, f32[4,34,8,128]{3,2,1,0:T(8,128)} %constant.2.clone.refs_2_), custom_call_target="tpu_custom_call" | custom-call | tf_op jit(solution)/shard_map/paradiag/pallas_call | solution.py:758
  47.5 0.8 %write_out.1 = f32[16,8,8,128]{3,2,1,0:T(8,128)} custom-call(f32[16,8,8,128]{3,2,1,0:T(8,128)S(1)} %paradiag.1.src), custom_call_target="tpu_custom_call" | custom-call | tf_op jit(solution)/shard_map/write_out/pallas_call | solution.py:796
